TPU v7x, 32 devices: a whole 2x2x4 slice. The times are simulated.
32 devices in a mesh: dp: 2 (over x), tp: 16 (over y, z, core).
Axes of the slice: x: 2, y: 2, z: 4, core: 2. Of those that a mesh axis runs over, the one named last changes fastest.
Arguments:
- x: bfloat16 [8192, 4096], P(('dp', 'tp')), parts along dimension 0
- dy: bfloat16 [8192, 4096], P(('dp', 'tp')), parts along dimension 0
- pre: bfloat16 [8192, 16384], P('dp', 'tp'), parts along dimension 0
- w_in: bfloat16 [4096, 16384], P(None, 'tp')
- w_down: bfloat16 [16384, 4096], P('tp')
Outputs:
- output 1: bfloat16 [8192, 4096], P(('dp', 'tp')), parts along dimension 0
- output 2: bfloat16 [8192, 16384], P('dp', 'tp'), parts along dimension 0
- output 3: bfloat16 [32768, 4096], P(('dp', 'tp')), parts along dimension 0
There are 2 independent parts. A program takes and returns all parts, laid end to end along the dimension named above; an argument that names none is the same for every part.
All inputs are finite; a program needn't handle non-finite values.
Results may differ from a plain program's by a relative error of at most 0.012.
Values are sent between devices in bfloat16 or wider.
A program may use at most 2 GiB of HBM per device.

v0:
```python
import jax
import jax.numpy as jnp


def act(pre):
    return jax.nn.gelu(pre)


def solution(mesh):
    def step(x, dy, pre, w_in, w_down):
        hidden, back = jax.vjp(act, pre.astype(jnp.float32))
        d_hidden = jnp.dot(dy, w_down.T, preferred_element_type=jnp.float32)
        d_pre = back(d_hidden)[0].astype(jnp.bfloat16)
        dx = jnp.dot(d_pre, w_in.T)
        groups = mesh.shape["dp"]

        def by_group(a, b):
            a, b = (t.reshape(groups, -1, t.shape[-1]) for t in (a, b))
            product = jnp.einsum("gta,gtb->gab", a, b, preferred_element_type=jnp.float32)
            return product.astype(jnp.bfloat16).reshape(-1, b.shape[-1])

        return dx, by_group(x, d_pre), by_group(hidden.astype(jnp.bfloat16), dy)

    return step
```

profile of v0, /device:TPU:0, one launch (start us, length us, event | category | flops | bytes accessed | tf_op | source)
XLA Modules:
  0.0 1358.1 jit_solution(5625656785479211205)
XLA Ops:
  7.2 3.2 copy.29
  10.4 3.2 copy.30
  13.6 170.8 %all-gather.5.cloned.1.call-done = bf16[4096,4096]{1,0:T(8,128)(2,1)} async-done(((bf16[256,4096]{1,0:T(8,128)(2,1)}), bf16[4096,4096]{1,0:T(8,128)(2,1)}) %all-gather.5.cloned.1.call-update) | async-done | bytes 33554448 | tf_op args[1]
  184.4 53.0 %fusion.40 = (bf16[1,4096,1024]{2,1,0:T(8,128)(2,1)}, bf16[4096,1024]{1,0:T(8,128)(2,1)}) fusion(bf16[4096,1024]{1,0:T(8,128)(2,1)} %param.6, bf16[4096,4096]{1,0:T(8,128)(2,1)} %all-gather.5.cloned.1.call-done, bf16[1024,4096]{1,0:T(8,128)(2,1)} %param.5), kind=kOutput, calls=%fused_computation.57 | convolution fusion | flops 34456207360 | bytes 67108864 | tf_op jit(solution)/dot_general | solution.py:12
  237.4 43.1 %fusion.41 = bf16[4096,4096]{1,0:T(8,128)(2,1)} fusion(bf16[4096,1024]{1,0:T(8,128)(2,1)} %get-tuple-element.81, bf16[4096,1024]{1,0:T(8,128)(2,1)} %param.7), kind=kOutput, calls=%fused_computation.60 | convolution fusion | flops 34359738368 | bytes 50331648 | tf_op jit(solution)/dot_general | solution.py:14
  282.3 11.6 copy
  293.9 14.9 %collective-permute-done.8 = bf16[1,1,256,4096]{3,2,1,0:T(8,128)(2,1)} collective-permute-done((bf16[1,1,256,4096]{3,2,1,0:T(8,128)(2,1)}, bf16[1,1,256,4096]{3,2,1,0:T(8,128)(2,1)}, u32[]{:S(2)}, u32[]{:S(2)}) %collective-permute-start.8) | collective-permute-done | bytes 2097184 | tf_op jit(solution)/gta,gtb->gab/dot_general | solution.py:19
  308.8 607.5 %while.4 = (bf16[1,4096,1024]{1,2,0:T(8,128)(2,1)}, bf16[1,1,256,4096]{3,2,1,0:T(8,128)(2,1)}, f32[1,1024,4096]{2,1,0:T(8,128)}, bf16[1,1,256,4096]{3,2,1,0:T(8,...) while((bf16[1,4096,1024]{1,2,0:T(8,128)(2,1)}, ...), condition=%wide.windowed_dot_general_cond_ag.clone, body=%wide.windowed_dot_general_body_ag.clone.sunk | while | flops 8610906112 | bytes 134218288 | solution.py:19
  310.4 3.1 copy.9
  315.9 57.5 %collective-permute-done = bf16[1,1,256,4096]{3,2,1,0:T(8,128)(2,1)} collective-permute-done((bf16[1,1,256,4096]{3,2,1,0:T(8,128)(2,1)S(1)}, bf16[1,1,256,4096]{3,2,1,0:T(8,128)(2,1)}, u32[]{:S(2)}, u32[]{:S(2)}) %collective-permute-start) | collective-permute-done | bytes 2097184 | tf_op jit(solution)/gta,gtb->gab/dot_general | solution.py:19
  373.5 4.6 collective-permute-start.1
  378.1 66.4 %collective-permute-done.2 = bf16[1,1,256,4096]{3,2,1,0:T(8,128)(2,1)} collective-permute-done((bf16[1,1,256,4096]{3,2,1,0:T(8,128)(2,1)}, bf16[1,1,256,4096]{3,2,1,0:T(8,128)(2,1)}, u32[]{:S(2)}, u32[]{:S(2)}) %collective-permute-start.2) | collective-permute-done | bytes 2097184 | tf_op jit(solution)/gta,gtb->gab/dot_general | solution.py:19
  444.5 12.3 fusion.54
  457.4 12.9 bitcast_add_fusion.6
  470.3 50.3 %collective-permute-done.3 = bf16[1,1,256,4096]{3,2,1,0:T(8,128)(2,1)} collective-permute-done((bf16[1,1,256,4096]{3,2,1,0:T(8,128)(2,1)}, bf16[1,1,256,4096]{3,2,1,0:T(8,128)(2,1)}, u32[]{:S(2)}, u32[]{:S(2)}) %collective-permute-start.3) | collective-permute-done | bytes 2097184 | tf_op jit(solution)/gta,gtb->gab/dot_general | solution.py:19
  527.8 68.5 %collective-permute-done = bf16[1,1,256,4096]{3,2,1,0:T(8,128)(2,1)} collective-permute-done((bf16[1,1,256,4096]{3,2,1,0:T(8,128)(2,1)S(1)}, bf16[1,1,256,4096]{3,2,1,0:T(8,128)(2,1)}, u32[]{:S(2)}, u32[]{:S(2)}) %collective-permute-start) | collective-permute-done | bytes 2097184 | tf_op jit(solution)/gta,gtb->gab/dot_general | solution.py:19
  596.3 4.6 collective-permute-start.1
  600.9 11.9 collective-permute-done.2
  612.8 12.3 fusion.54
  625.7 20.7 %bitcast_add_fusion.6 = f32[1,1024,4096]{2,1,0:T(8,128)} fusion(f32[1024,4096,1]{1,0,2:T(8,128)} %fusion.54, f32[1,1024,4096]{2,1,0:T(8,128)} %get-tuple-element.157, pred[]{:T(512)S(6)} %compare.12, bf16[1,1,256,4096]{3,2,1,0:T(8,128)(2,1)} %collective-permute-done.2, bf16[1,1,256,4096]{3,2,1,0:T(8,128)(2,1)} %collective-permute-done, ...), kind=kOutput, calls=%fused_computation.4.clone.1 | convolution fusion | flops 4311744512 | bytes 62914568 | tf_op jit(solution)/gta,gtb->gab/dot_general | solution.py:19
  646.5 11.7 collective-permute-done.3
  665.3 63.6 %collective-permute-done = bf16[1,1,256,4096]{3,2,1,0:T(8,128)(2,1)} collective-permute-done((bf16[1,1,256,4096]{3,2,1,0:T(8,128)(2,1)S(1)}, bf16[1,1,256,4096]{3,2,1,0:T(8,128)(2,1)}, u32[]{:S(2)}, u32[]{:S(2)}) %collective-permute-start) | collective-permute-done | bytes 2097184 | tf_op jit(solution)/gta,gtb->gab/dot_general | solution.py:19
  728.9 4.6 collective-permute-start.1
  733.5 10.6 collective-permute-done.2
  744.2 12.3 fusion.54
  757.1 20.7 %bitcast_add_fusion.6 = f32[1,1024,4096]{2,1,0:T(8,128)} fusion(f32[1024,4096,1]{1,0,2:T(8,128)} %fusion.54, f32[1,1024,4096]{2,1,0:T(8,128)} %get-tuple-element.157, pred[]{:T(512)S(6)} %compare.12, bf16[1,1,256,4096]{3,2,1,0:T(8,128)(2,1)} %collective-permute-done.2, bf16[1,1,256,4096]{3,2,1,0:T(8,128)(2,1)} %collective-permute-done, ...), kind=kOutput, calls=%fused_computation.4.clone.1 | convolution fusion | flops 4311744512 | bytes 62914568 | tf_op jit(solution)/gta,gtb->gab/dot_general | solution.py:19
  777.8 38.3 %collective-permute-done.1 = bf16[1,1,256,4096]{3,2,1,0:T(8,128)(2,1)} collective-permute-done((bf16[1,1,256,4096]{3,2,1,0:T(8,128)(2,1)}, bf16[1,1,256,4096]{3,2,1,0:T(8,128)(2,1)}, u32[]{:S(2)}, u32[]{:S(2)}) %collective-permute-start.1) | collective-permute-done | bytes 2097184 | tf_op jit(solution)/gta,gtb->gab/dot_general | solution.py:19
  817.7 4.6 collective-permute-start
  827.4 38.5 %collective-permute-done = bf16[1,1,256,4096]{3,2,1,0:T(8,128)(2,1)} collective-permute-done((bf16[1,1,256,4096]{3,2,1,0:T(8,128)(2,1)S(1)}, bf16[1,1,256,4096]{3,2,1,0:T(8,128)(2,1)}, u32[]{:S(2)}, u32[]{:S(2)}) %collective-permute-start) | collective-permute-done | bytes 2097184 | tf_op jit(solution)/gta,gtb->gab/dot_general | solution.py:19
  865.9 4.6 collective-permute-start.1
  872.8 12.3 fusion.54
  885.7 20.7 %bitcast_add_fusion.6 = f32[1,1024,4096]{2,1,0:T(8,128)} fusion(f32[1024,4096,1]{1,0,2:T(8,128)} %fusion.54, f32[1,1024,4096]{2,1,0:T(8,128)} %get-tuple-element.157, pred[]{:T(512)S(6)} %compare.12, bf16[1,1,256,4096]{3,2,1,0:T(8,128)(2,1)} %collective-permute-done.2, bf16[1,1,256,4096]{3,2,1,0:T(8,128)(2,1)} %collective-permute-done, ...), kind=kOutput, calls=%fused_computation.4.clone.1 | convolution fusion | flops 4311744512 | bytes 62914568 | tf_op jit(solution)/gta,gtb->gab/dot_general | solution.py:19
  906.4 9.9 collective-permute-done.1
  916.3 13.8 %copy.1 = bf16[1,1024,4096]{1,2,0:T(8,128)(2,1)} copy(f32[1,1024,4096]{2,1,0:T(8,128)} %get-tuple-element.12) | data formatting | bytes 25165824 | tf_op jit(solution)/gta,gtb->gab/dot_general | solution.py:19
  930.1 11.4 copy.2
  941.5 400.8 %while.5 = (bf16[1,4096,1024]{1,2,0:T(8,128)(2,1)}, bf16[1,1,256,4096]{3,2,1,0:T(8,128)(2,1)}, f32[1,1024,4096]{2,1,0:T(8,128)}, bf16[1,1,256,4096]{3,2,1,0:T(8,...) while((bf16[1,4096,1024]{1,2,0:T(8,128)(2,1)}, ...), condition=%wide.windowed_dot_general_cond_ag.1.clone, body=%wide.windowed_dot_general_body_ag.1.clone.sunk | while | flops 8610906112 | bytes 134218288 | solution.py:19
  943.1 4.6 collective-permute-start.4
  952.6 40.9 %collective-permute-done.4 = bf16[1,1,256,4096]{3,2,1,0:T(8,128)(2,1)} collective-permute-done((bf16[1,1,256,4096]{3,2,1,0:T(8,128)(2,1)S(1)}, bf16[1,1,256,4096]{3,2,1,0:T(8,128)(2,1)}, u32[]{:S(2)}, u32[]{:S(2)}) %collective-permute-start.4) | collective-permute-done | bytes 2097184 | tf_op jit(solution)/gta,gtb->gab/dot_general | solution.py:19
  993.6 4.6 collective-permute-start.5
  998.2 12.2 fusion.57
  1011.0 12.9 bitcast_add_fusion.7
  1023.9 17.8 %collective-permute-done.5 = bf16[1,1,256,4096]{3,2,1,0:T(8,128)(2,1)} collective-permute-done((bf16[1,1,256,4096]{3,2,1,0:T(8,128)(2,1)}, bf16[1,1,256,4096]{3,2,1,0:T(8,128)(2,1)}, u32[]{:S(2)}, u32[]{:S(2)}) %collective-permute-start.5) | collective-permute-done | bytes 2097184 | tf_op jit(solution)/gta,gtb->gab/dot_general | solution.py:19
  1043.3 4.6 collective-permute-start.4
  1052.8 39.5 %collective-permute-done.4 = bf16[1,1,256,4096]{3,2,1,0:T(8,128)(2,1)} collective-permute-done((bf16[1,1,256,4096]{3,2,1,0:T(8,128)(2,1)S(1)}, bf16[1,1,256,4096]{3,2,1,0:T(8,128)(2,1)}, u32[]{:S(2)}, u32[]{:S(2)}) %collective-permute-start.4) | collective-permute-done | bytes 2097184 | tf_op jit(solution)/gta,gtb->gab/dot_general | solution.py:19
  1092.3 4.6 collective-permute-start.5
  1098.3 12.2 fusion.57
  1111.1 20.7 %bitcast_add_fusion.7 = f32[1,1024,4096]{2,1,0:T(8,128)} fusion(f32[1024,4096,1]{1,0,2:T(8,128)} %fusion.57, f32[1,1024,4096]{2,1,0:T(8,128)} %get-tuple-element.190, pred[]{:T(512)S(6)} %compare.13, bf16[1,1,256,4096]{3,2,1,0:T(8,128)(2,1)} %collective-permute-done.6, bf16[1,1,256,4096]{3,2,1,0:T(8,128)(2,1)} %collective-permute-done.4, ...), kind=kOutput, calls=%fused_computation.25.clone.1 | convolution fusion | flops 4311744512 | bytes 62914568 | tf_op jit(solution)/gta,gtb->gab/dot_general | solution.py:19
  1131.8 6.7 collective-permute-done.5
  1140.1 4.6 collective-permute-start.4
  1149.6 39.5 %collective-permute-done.4 = bf16[1,1,256,4096]{3,2,1,0:T(8,128)(2,1)} collective-permute-done((bf16[1,1,256,4096]{3,2,1,0:T(8,128)(2,1)S(1)}, bf16[1,1,256,4096]{3,2,1,0:T(8,128)(2,1)}, u32[]{:S(2)}, u32[]{:S(2)}) %collective-permute-start.4) | collective-permute-done | bytes 2097184 | tf_op jit(solution)/gta,gtb->gab/dot_general | solution.py:19
  1189.1 4.6 collective-permute-start.5
  1193.7 4.2 collective-permute-done.6
  1197.9 12.2 fusion.57
  1210.6 20.7 %bitcast_add_fusion.7 = f32[1,1024,4096]{2,1,0:T(8,128)} fusion(f32[1024,4096,1]{1,0,2:T(8,128)} %fusion.57, f32[1,1024,4096]{2,1,0:T(8,128)} %get-tuple-element.190, pred[]{:T(512)S(6)} %compare.13, bf16[1,1,256,4096]{3,2,1,0:T(8,128)(2,1)} %collective-permute-done.6, bf16[1,1,256,4096]{3,2,1,0:T(8,128)(2,1)} %collective-permute-done.4, ...), kind=kOutput, calls=%fused_computation.25.clone.1 | convolution fusion | flops 4311744512 | bytes 62914568 | tf_op jit(solution)/gta,gtb->gab/dot_general | solution.py:19
  1231.4 4.0 collective-permute-done.5
  1235.4 7.9 collective-permute-done.7
  1250.2 37.7 %collective-permute-done.4 = bf16[1,1,256,4096]{3,2,1,0:T(8,128)(2,1)} collective-permute-done((bf16[1,1,256,4096]{3,2,1,0:T(8,128)(2,1)S(1)}, bf16[1,1,256,4096]{3,2,1,0:T(8,128)(2,1)}, u32[]{:S(2)}, u32[]{:S(2)}) %collective-permute-start.4) | collective-permute-done | bytes 2097184 | tf_op jit(solution)/gta,gtb->gab/dot_general | solution.py:19
  1287.9 4.6 collective-permute-start.5
  1292.5 4.4 collective-permute-done.6
  1296.9 12.2 fusion.57
  1309.7 20.7 %bitcast_add_fusion.7 = f32[1,1024,4096]{2,1,0:T(8,128)} fusion(f32[1024,4096,1]{1,0,2:T(8,128)} %fusion.57, f32[1,1024,4096]{2,1,0:T(8,128)} %get-tuple-element.190, pred[]{:T(512)S(6)} %compare.13, bf16[1,1,256,4096]{3,2,1,0:T(8,128)(2,1)} %collective-permute-done.6, bf16[1,1,256,4096]{3,2,1,0:T(8,128)(2,1)} %collective-permute-done.4, ...), kind=kOutput, calls=%fused_computation.25.clone.1 | convolution fusion | flops 4311744512 | bytes 62914568 | tf_op jit(solution)/gta,gtb->gab/dot_general | solution.py:19
  1330.4 7.9 collective-permute-done.5
  1338.3 4.0 collective-permute-done.7
  1342.3 9.0 convert_bitcast_fusion
  (64 shorter events, 47.0 us)
Async XLA Ops:
  7.2 177.3 %all-gather.5.cloned.1.call-start = ((), (), s32[]{:S(2)}) async-start(), calls=%async_computation.1 | async-start | bytes 35651584 | tf_op args[1]
  13.6 1337.7 %reduce-scatter.4.cloned.1.call-start = ((), (), s32[]{:S(2)}) async-start(), calls=%async_computation.2 | async-start | bytes 35651584
  280.6 28.2 %collective-permute-start.8 = (bf16[1,1,256,4096]{3,2,1,0:T(8,128)(2,1)}, bf16[1,1,256,4096]{3,2,1,0:T(8,128)(2,1)}, u32[]{:S(2)}, u32[]{:S(2)}) collective-permute-start(bf16[1,1,256,4096]{3,2,1,0:T(8,128)(2,1)} %bitcast.2), channel_id=5, source_target_pairs={{0,1},{1,2},{2,3},{3,4},{4,5},{5,6},{6,7},{7,8},{8,9},{9,10},{10,1... | collective-permute-start | bytes 6291464 | tf_op jit(solution)/gta,gtb->gab/dot_general | solution.py:19
  280.9 660.6 %collective-permute-start.9 = (bf16[1,1,256,4096]{3,2,1,0:T(8,128)(2,1)}, bf16[1,1,256,4096]{3,2,1,0:T(8,128)(2,1)}, u32[]{:S(2)}, u32[]{:S(2)}) collective-permute-start(bf16[1,1,256,4096]{3,2,1,0:T(8,128)(2,1)} %bitcast.6), channel_id=11, source_target_pairs={{0,1},{1,2},{2,3},{3,4},{4,5},{5,6},{6,7},{7,8},{8,9},{9,10},{10,1... | collective-permute-start | bytes 6291464 | tf_op jit(solution)/gta,gtb->gab/dot_general | solution.py:19
  282.3 26.6 %copy-start = (u32[32]{0:T(128)S(1)}, u32[32]{0:T(128)}, u32[]{:S(2)}) copy-start(u32[32]{0:T(128)} %constant.246) | copy-start | bytes 388
  310.4 63.1 %collective-permute-start = (bf16[1,1,256,4096]{3,2,1,0:T(8,128)(2,1)S(1)}, bf16[1,1,256,4096]{3,2,1,0:T(8,128)(2,1)}, u32[]{:S(2)}, u32[]{:S(2)}) collective-permute-start(bf16[1,1,256,4096]{3,2,1,0:T(8,128)(2,1)S(1)} %copy.7), channel_id=6, source_target_pairs={{0,15},{1,0},{2,1},{3,2},{4,3},{5,4},{6,5},{7,6},{8,7},{9,8},{10,9... | collective-permute-start | bytes 6291464 | tf_op jit(solution)/gta,gtb->gab/dot_general | solution.py:19
  313.5 130.9 %collective-permute-start.2 = (bf16[1,1,256,4096]{3,2,1,0:T(8,128)(2,1)}, bf16[1,1,256,4096]{3,2,1,0:T(8,128)(2,1)}, u32[]{:S(2)}, u32[]{:S(2)}) collective-permute-start(bf16[1,1,256,4096]{3,2,1,0:T(8,128)(2,1)} %copy.9), channel_id=7, source_target_pairs={{0,1},{1,2},{2,3},{3,4},{4,5},{5,6},{6,7},{7,8},{8,9},{9,10},{10,1... | collective-permute-start | bytes 6291464 | tf_op jit(solution)/gta,gtb->gab/dot_general | solution.py:19
  373.5 96.9 %collective-permute-start.1 = (bf16[1,1,256,4096]{3,2,1,0:T(8,128)(2,1)}, bf16[1,1,256,4096]{3,2,1,0:T(8,128)(2,1)}, u32[]{:S(2)}, u32[]{:S(2)}) collective-permute-start(bf16[1,1,256,4096]{3,2,1,0:T(8,128)(2,1)} %collective-permute-done), channel_id=8, source_target_pairs={{0,15},{1,0},{2,1},{3,2},{4,3},{5,4},{6,5},{7,6},{8,7},{9,8},{10,9... | collective-permute-start | bytes 6291464 | tf_op jit(solution)/gta,gtb->gab/dot_general | solution.py:19
  444.5 76.2 %collective-permute-start.3 = (bf16[1,1,256,4096]{3,2,1,0:T(8,128)(2,1)}, bf16[1,1,256,4096]{3,2,1,0:T(8,128)(2,1)}, u32[]{:S(2)}, u32[]{:S(2)}) collective-permute-start(bf16[1,1,256,4096]{3,2,1,0:T(8,128)(2,1)} %collective-permute-done.2), channel_id=9, source_target_pairs={{0,1},{1,2},{2,3},{3,4},{4,5},{5,6},{6,7},{7,8},{8,9},{9,10},{10,1... | collective-permute-start | bytes 6291464 | tf_op jit(solution)/gta,gtb->gab/dot_general | solution.py:19
  522.2 74.0 %collective-permute-start = (bf16[1,1,256,4096]{3,2,1,0:T(8,128)(2,1)S(1)}, bf16[1,1,256,4096]{3,2,1,0:T(8,128)(2,1)}, u32[]{:S(2)}, u32[]{:S(2)}) collective-permute-start(bf16[1,1,256,4096]{3,2,1,0:T(8,128)(2,1)S(1)} %copy.7), channel_id=6, source_target_pairs={{0,15},{1,0},{2,1},{3,2},{4,3},{5,4},{6,5},{7,6},{8,7},{9,8},{10,9... | collective-permute-start | bytes 6291464 | tf_op jit(solution)/gta,gtb->gab/dot_general | solution.py:19
  525.4 87.5 %collective-permute-start.2 = (bf16[1,1,256,4096]{3,2,1,0:T(8,128)(2,1)}, bf16[1,1,256,4096]{3,2,1,0:T(8,128)(2,1)}, u32[]{:S(2)}, u32[]{:S(2)}) collective-permute-start(bf16[1,1,256,4096]{3,2,1,0:T(8,128)(2,1)} %copy.9), channel_id=7, source_target_pairs={{0,1},{1,2},{2,3},{3,4},{4,5},{5,6},{6,7},{7,8},{8,9},{9,10},{10,1... | collective-permute-start | bytes 6291464 | tf_op jit(solution)/gta,gtb->gab/dot_general | solution.py:19
  596.3 50.2 %collective-permute-start.1 = (bf16[1,1,256,4096]{3,2,1,0:T(8,128)(2,1)}, bf16[1,1,256,4096]{3,2,1,0:T(8,128)(2,1)}, u32[]{:S(2)}, u32[]{:S(2)}) collective-permute-start(bf16[1,1,256,4096]{3,2,1,0:T(8,128)(2,1)} %collective-permute-done), channel_id=8, source_target_pairs={{0,15},{1,0},{2,1},{3,2},{4,3},{5,4},{6,5},{7,6},{8,7},{9,8},{10,9... | collective-permute-start | bytes 6291464 | tf_op jit(solution)/gta,gtb->gab/dot_general | solution.py:19
  612.8 45.4 %collective-permute-start.3 = (bf16[1,1,256,4096]{3,2,1,0:T(8,128)(2,1)}, bf16[1,1,256,4096]{3,2,1,0:T(8,128)(2,1)}, u32[]{:S(2)}, u32[]{:S(2)}) collective-permute-start(bf16[1,1,256,4096]{3,2,1,0:T(8,128)(2,1)} %collective-permute-done.2), channel_id=9, source_target_pairs={{0,1},{1,2},{2,3},{3,4},{4,5},{5,6},{6,7},{7,8},{8,9},{9,10},{10,1... | collective-permute-start | bytes 6291464 | tf_op jit(solution)/gta,gtb->gab/dot_general | solution.py:19
  659.8 69.1 %collective-permute-start = (bf16[1,1,256,4096]{3,2,1,0:T(8,128)(2,1)S(1)}, bf16[1,1,256,4096]{3,2,1,0:T(8,128)(2,1)}, u32[]{:S(2)}, u32[]{:S(2)}) collective-permute-start(bf16[1,1,256,4096]{3,2,1,0:T(8,128)(2,1)S(1)} %copy.7), channel_id=6, source_target_pairs={{0,15},{1,0},{2,1},{3,2},{4,3},{5,4},{6,5},{7,6},{8,7},{9,8},{10,9... | collective-permute-start | bytes 6291464 | tf_op jit(solution)/gta,gtb->gab/dot_general | solution.py:19
  662.9 81.2 %collective-permute-start.2 = (bf16[1,1,256,4096]{3,2,1,0:T(8,128)(2,1)}, bf16[1,1,256,4096]{3,2,1,0:T(8,128)(2,1)}, u32[]{:S(2)}, u32[]{:S(2)}) collective-permute-start(bf16[1,1,256,4096]{3,2,1,0:T(8,128)(2,1)} %copy.9), channel_id=7, source_target_pairs={{0,1},{1,2},{2,3},{3,4},{4,5},{5,6},{6,7},{7,8},{8,9},{9,10},{10,1... | collective-permute-start | bytes 6291464 | tf_op jit(solution)/gta,gtb->gab/dot_general | solution.py:19
  728.9 87.2 %collective-permute-start.1 = (bf16[1,1,256,4096]{3,2,1,0:T(8,128)(2,1)}, bf16[1,1,256,4096]{3,2,1,0:T(8,128)(2,1)}, u32[]{:S(2)}, u32[]{:S(2)}) collective-permute-start(bf16[1,1,256,4096]{3,2,1,0:T(8,128)(2,1)} %collective-permute-done), channel_id=8, source_target_pairs={{0,15},{1,0},{2,1},{3,2},{4,3},{5,4},{6,5},{7,6},{8,7},{9,8},{10,9... | collective-permute-start | bytes 6291464 | tf_op jit(solution)/gta,gtb->gab/dot_general | solution.py:19
  744.2 72.0 %collective-permute-start.3 = (bf16[1,1,256,4096]{3,2,1,0:T(8,128)(2,1)}, bf16[1,1,256,4096]{3,2,1,0:T(8,128)(2,1)}, u32[]{:S(2)}, u32[]{:S(2)}) collective-permute-start(bf16[1,1,256,4096]{3,2,1,0:T(8,128)(2,1)} %collective-permute-done.2), channel_id=9, source_target_pairs={{0,1},{1,2},{2,3},{3,4},{4,5},{5,6},{6,7},{7,8},{8,9},{9,10},{10,1... | collective-permute-start | bytes 6291464 | tf_op jit(solution)/gta,gtb->gab/dot_general | solution.py:19
  817.7 48.2 %collective-permute-start = (bf16[1,1,256,4096]{3,2,1,0:T(8,128)(2,1)S(1)}, bf16[1,1,256,4096]{3,2,1,0:T(8,128)(2,1)}, u32[]{:S(2)}, u32[]{:S(2)}) collective-permute-start(bf16[1,1,256,4096]{3,2,1,0:T(8,128)(2,1)S(1)} %copy.7), channel_id=6, source_target_pairs={{0,15},{1,0},{2,1},{3,2},{4,3},{5,4},{6,5},{7,6},{8,7},{9,8},{10,9... | collective-permute-start | bytes 6291464 | tf_op jit(solution)/gta,gtb->gab/dot_general | solution.py:19
  825.5 47.3 %collective-permute-start.2 = (bf16[1,1,256,4096]{3,2,1,0:T(8,128)(2,1)}, bf16[1,1,256,4096]{3,2,1,0:T(8,128)(2,1)}, u32[]{:S(2)}, u32[]{:S(2)}) collective-permute-start(bf16[1,1,256,4096]{3,2,1,0:T(8,128)(2,1)} %copy.9), channel_id=7, source_target_pairs={{0,1},{1,2},{2,3},{3,4},{4,5},{5,6},{6,7},{7,8},{8,9},{9,10},{10,1... | collective-permute-start | bytes 6291464 | tf_op jit(solution)/gta,gtb->gab/dot_general | solution.py:19
  865.9 50.4 %collective-permute-start.1 = (bf16[1,1,256,4096]{3,2,1,0:T(8,128)(2,1)}, bf16[1,1,256,4096]{3,2,1,0:T(8,128)(2,1)}, u32[]{:S(2)}, u32[]{:S(2)}) collective-permute-start(bf16[1,1,256,4096]{3,2,1,0:T(8,128)(2,1)} %collective-permute-done), channel_id=8, source_target_pairs={{0,15},{1,0},{2,1},{3,2},{4,3},{5,4},{6,5},{7,6},{8,7},{9,8},{10,9... | collective-permute-start | bytes 6291464 | tf_op jit(solution)/gta,gtb->gab/dot_general | solution.py:19
  872.8 43.5 %collective-permute-start.3 = (bf16[1,1,256,4096]{3,2,1,0:T(8,128)(2,1)}, bf16[1,1,256,4096]{3,2,1,0:T(8,128)(2,1)}, u32[]{:S(2)}, u32[]{:S(2)}) collective-permute-start(bf16[1,1,256,4096]{3,2,1,0:T(8,128)(2,1)} %collective-permute-done.2), channel_id=9, source_target_pairs={{0,1},{1,2},{2,3},{3,4},{4,5},{5,6},{6,7},{7,8},{8,9},{9,10},{10,1... | collective-permute-start | bytes 6291464 | tf_op jit(solution)/gta,gtb->gab/dot_general | solution.py:19
  943.1 50.4 %collective-permute-start.4 = (bf16[1,1,256,4096]{3,2,1,0:T(8,128)(2,1)S(1)}, bf16[1,1,256,4096]{3,2,1,0:T(8,128)(2,1)}, u32[]{:S(2)}, u32[]{:S(2)}) collective-permute-start(bf16[1,1,256,4096]{3,2,1,0:T(8,128)(2,1)S(1)} %copy.19), channel_id=12, source_target_pairs={{0,15},{1,0},{2,1},{3,2},{4,3},{5,4},{6,5},{7,6},{8,7},{9,8},{10,9... | collective-permute-start | bytes 6291464 | tf_op jit(solution)/gta,gtb->gab/dot_general | solution.py:19
  950.9 47.3 %collective-permute-start.6 = (bf16[1,1,256,4096]{3,2,1,0:T(8,128)(2,1)}, bf16[1,1,256,4096]{3,2,1,0:T(8,128)(2,1)}, u32[]{:S(2)}, u32[]{:S(2)}) collective-permute-start(bf16[1,1,256,4096]{3,2,1,0:T(8,128)(2,1)} %copy.21), channel_id=13, source_target_pairs={{0,1},{1,2},{2,3},{3,4},{4,5},{5,6},{6,7},{7,8},{8,9},{9,10},{10,1... | collective-permute-start | bytes 6291464 | tf_op jit(solution)/gta,gtb->gab/dot_general | solution.py:19
  993.6 48.1 %collective-permute-start.5 = (bf16[1,1,256,4096]{3,2,1,0:T(8,128)(2,1)}, bf16[1,1,256,4096]{3,2,1,0:T(8,128)(2,1)}, u32[]{:S(2)}, u32[]{:S(2)}) collective-permute-start(bf16[1,1,256,4096]{3,2,1,0:T(8,128)(2,1)} %collective-permute-done.4), channel_id=14, source_target_pairs={{0,15},{1,0},{2,1},{3,2},{4,3},{5,4},{6,5},{7,6},{8,7},{9,8},{10,9... | collective-permute-start | bytes 6291464 | tf_op jit(solution)/gta,gtb->gab/dot_general | solution.py:19
  998.2 43.5 %collective-permute-start.7 = (bf16[1,1,256,4096]{3,2,1,0:T(8,128)(2,1)}, bf16[1,1,256,4096]{3,2,1,0:T(8,128)(2,1)}, u32[]{:S(2)}, u32[]{:S(2)}) collective-permute-start(bf16[1,1,256,4096]{3,2,1,0:T(8,128)(2,1)} %collective-permute-done.6), channel_id=15, source_target_pairs={{0,1},{1,2},{2,3},{3,4},{4,5},{5,6},{6,7},{7,8},{8,9},{9,10},{10,1... | collective-permute-start | bytes 6291464 | tf_op jit(solution)/gta,gtb->gab/dot_general | solution.py:19
  1043.3 49.0 %collective-permute-start.4 = (bf16[1,1,256,4096]{3,2,1,0:T(8,128)(2,1)S(1)}, bf16[1,1,256,4096]{3,2,1,0:T(8,128)(2,1)}, u32[]{:S(2)}, u32[]{:S(2)}) collective-permute-start(bf16[1,1,256,4096]{3,2,1,0:T(8,128)(2,1)S(1)} %copy.19), channel_id=12, source_target_pairs={{0,15},{1,0},{2,1},{3,2},{4,3},{5,4},{6,5},{7,6},{8,7},{9,8},{10,9... | collective-permute-start | bytes 6291464 | tf_op jit(solution)/gta,gtb->gab/dot_general | solution.py:19
  1051.1 47.3 %collective-permute-start.6 = (bf16[1,1,256,4096]{3,2,1,0:T(8,128)(2,1)}, bf16[1,1,256,4096]{3,2,1,0:T(8,128)(2,1)}, u32[]{:S(2)}, u32[]{:S(2)}) collective-permute-start(bf16[1,1,256,4096]{3,2,1,0:T(8,128)(2,1)} %copy.21), channel_id=13, source_target_pairs={{0,1},{1,2},{2,3},{3,4},{4,5},{5,6},{6,7},{7,8},{8,9},{9,10},{10,1... | collective-permute-start | bytes 6291464 | tf_op jit(solution)/gta,gtb->gab/dot_general | solution.py:19
  1092.3 46.3 %collective-permute-start.5 = (bf16[1,1,256,4096]{3,2,1,0:T(8,128)(2,1)}, bf16[1,1,256,4096]{3,2,1,0:T(8,128)(2,1)}, u32[]{:S(2)}, u32[]{:S(2)}) collective-permute-start(bf16[1,1,256,4096]{3,2,1,0:T(8,128)(2,1)} %collective-permute-done.4), channel_id=14, source_target_pairs={{0,15},{1,0},{2,1},{3,2},{4,3},{5,4},{6,5},{7,6},{8,7},{9,8},{10,9... | collective-permute-start | bytes 6291464 | tf_op jit(solution)/gta,gtb->gab/dot_general | solution.py:19
  1098.3 40.2 %collective-permute-start.7 = (bf16[1,1,256,4096]{3,2,1,0:T(8,128)(2,1)}, bf16[1,1,256,4096]{3,2,1,0:T(8,128)(2,1)}, u32[]{:S(2)}, u32[]{:S(2)}) collective-permute-start(bf16[1,1,256,4096]{3,2,1,0:T(8,128)(2,1)} %collective-permute-done.6), channel_id=15, source_target_pairs={{0,1},{1,2},{2,3},{3,4},{4,5},{5,6},{6,7},{7,8},{8,9},{9,10},{10,1... | collective-permute-start | bytes 6291464 | tf_op jit(solution)/gta,gtb->gab/dot_general | solution.py:19
  1140.1 49.0 %collective-permute-start.4 = (bf16[1,1,256,4096]{3,2,1,0:T(8,128)(2,1)S(1)}, bf16[1,1,256,4096]{3,2,1,0:T(8,128)(2,1)}, u32[]{:S(2)}, u32[]{:S(2)}) collective-permute-start(bf16[1,1,256,4096]{3,2,1,0:T(8,128)(2,1)S(1)} %copy.19), channel_id=12, source_target_pairs={{0,15},{1,0},{2,1},{3,2},{4,3},{5,4},{6,5},{7,6},{8,7},{9,8},{10,9... | collective-permute-start | bytes 6291464 | tf_op jit(solution)/gta,gtb->gab/dot_general | solution.py:19
  1147.9 50.0 %collective-permute-start.6 = (bf16[1,1,256,4096]{3,2,1,0:T(8,128)(2,1)}, bf16[1,1,256,4096]{3,2,1,0:T(8,128)(2,1)}, u32[]{:S(2)}, u32[]{:S(2)}) collective-permute-start(bf16[1,1,256,4096]{3,2,1,0:T(8,128)(2,1)} %copy.21), channel_id=13, source_target_pairs={{0,1},{1,2},{2,3},{3,4},{4,5},{5,6},{6,7},{7,8},{8,9},{9,10},{10,1... | collective-permute-start | bytes 6291464 | tf_op jit(solution)/gta,gtb->gab/dot_general | solution.py:19
  1189.1 46.3 %collective-permute-start.5 = (bf16[1,1,256,4096]{3,2,1,0:T(8,128)(2,1)}, bf16[1,1,256,4096]{3,2,1,0:T(8,128)(2,1)}, u32[]{:S(2)}, u32[]{:S(2)}) collective-permute-start(bf16[1,1,256,4096]{3,2,1,0:T(8,128)(2,1)} %collective-permute-done.4), channel_id=14, source_target_pairs={{0,15},{1,0},{2,1},{3,2},{4,3},{5,4},{6,5},{7,6},{8,7},{9,8},{10,9... | collective-permute-start | bytes 6291464 | tf_op jit(solution)/gta,gtb->gab/dot_general | solution.py:19
  1197.9 45.4 %collective-permute-start.7 = (bf16[1,1,256,4096]{3,2,1,0:T(8,128)(2,1)}, bf16[1,1,256,4096]{3,2,1,0:T(8,128)(2,1)}, u32[]{:S(2)}, u32[]{:S(2)}) collective-permute-start(bf16[1,1,256,4096]{3,2,1,0:T(8,128)(2,1)} %collective-permute-done.6), channel_id=15, source_target_pairs={{0,1},{1,2},{2,3},{3,4},{4,5},{5,6},{6,7},{7,8},{8,9},{9,10},{10,1... | collective-permute-start | bytes 6291464 | tf_op jit(solution)/gta,gtb->gab/dot_general | solution.py:19
  1244.8 43.1 %collective-permute-start.4 = (bf16[1,1,256,4096]{3,2,1,0:T(8,128)(2,1)S(1)}, bf16[1,1,256,4096]{3,2,1,0:T(8,128)(2,1)}, u32[]{:S(2)}, u32[]{:S(2)}) collective-permute-start(bf16[1,1,256,4096]{3,2,1,0:T(8,128)(2,1)S(1)} %copy.19), channel_id=12, source_target_pairs={{0,15},{1,0},{2,1},{3,2},{4,3},{5,4},{6,5},{7,6},{8,7},{9,8},{10,9... | collective-permute-start | bytes 6291464 | tf_op jit(solution)/gta,gtb->gab/dot_general | solution.py:19
  1248.0 49.0 %collective-permute-start.6 = (bf16[1,1,256,4096]{3,2,1,0:T(8,128)(2,1)}, bf16[1,1,256,4096]{3,2,1,0:T(8,128)(2,1)}, u32[]{:S(2)}, u32[]{:S(2)}) collective-permute-start(bf16[1,1,256,4096]{3,2,1,0:T(8,128)(2,1)} %copy.21), channel_id=13, source_target_pairs={{0,1},{1,2},{2,3},{3,4},{4,5},{5,6},{6,7},{7,8},{8,9},{9,10},{10,1... | collective-permute-start | bytes 6291464 | tf_op jit(solution)/gta,gtb->gab/dot_general | solution.py:19
  1287.9 50.4 %collective-permute-start.5 = (bf16[1,1,256,4096]{3,2,1,0:T(8,128)(2,1)}, bf16[1,1,256,4096]{3,2,1,0:T(8,128)(2,1)}, u32[]{:S(2)}, u32[]{:S(2)}) collective-permute-start(bf16[1,1,256,4096]{3,2,1,0:T(8,128)(2,1)} %collective-permute-done.4), channel_id=14, source_target_pairs={{0,15},{1,0},{2,1},{3,2},{4,3},{5,4},{6,5},{7,6},{8,7},{9,8},{10,9... | collective-permute-start | bytes 6291464 | tf_op jit(solution)/gta,gtb->gab/dot_general | solution.py:19
  1296.9 45.4 %collective-permute-start.7 = (bf16[1,1,256,4096]{3,2,1,0:T(8,128)(2,1)}, bf16[1,1,256,4096]{3,2,1,0:T(8,128)(2,1)}, u32[]{:S(2)}, u32[]{:S(2)}) collective-permute-start(bf16[1,1,256,4096]{3,2,1,0:T(8,128)(2,1)} %collective-permute-done.6), channel_id=15, source_target_pairs={{0,1},{1,2},{2,3},{3,4},{4,5},{5,6},{6,7},{7,8},{8,9},{9,10},{10,1... | collective-permute-start | bytes 6291464 | tf_op jit(solution)/gta,gtb->gab/dot_general | solution.py:19
Sparse Core Ops, SparseCore 0:
  13.7 170.6 all-gather.4
  280.7 529.6 reduce-scatter.3
where the time goes:
time: 1360 us
  waiting for transfers between devices  831 us (61%)
  matrix products  344 us (25%)
  local copies, waits for them, and re-layouts  85.8 us (6%)
  starting transfers between devices  59.3 us (4%)
  loops' own time  14.5 us (1%)
  between operations  14 us (1%)
    dot_general x34, waiting for transfers between devices, by_group(): jnp.einsum('gta,gtb->gab', a, b, preferred_element_type=jnp.float32)  660 us
    dot_general x16, matrix products, by_group(): jnp.einsum('gta,gtb->gab', a, b, preferred_element_type=jnp.float32)  248 us
    unnamed x4, waiting for transfers between devices  171 us
    dot_general x34, starting transfers between devices, by_group(): jnp.einsum('gta,gtb->gab', a, b, preferred_element_type=jnp.float32)  59.2 us
    dot_general x1, matrix products, step(): d_hidden = jnp.dot(dy, w_down.T, preferred_element_type=jnp.float32)  53 us
    dot_general x1, matrix products, step(): dx = jnp.dot(d_pre, w_in.T)  43.1 us
    dot_general x16, local copies, waits for them, and re-layouts  37.8 us
    unnamed x6, local copies, waits for them, and re-layouts  29.3 us
  transfers between devices with their start and end apart: 36, of which 27 were waited for; matrix products, arithmetic and copies ran while one was open for 25% of the time, Pallas kernels for 0%

commit v1 on v0

v1 whole, which is shorter than its diff:
```python
import functools

import jax
import jax.numpy as jnp
import numpy as np
from jax import lax
from jax.experimental import pallas as pl
from jax.experimental.pallas import tpu as pltpu
from jax.sharding import PartitionSpec as P

MESH = pl.DeviceIdType.MESH
F32, BF16 = jnp.float32, jnp.bfloat16
D = 4096
FL = 1024
SH = 256
CHUNKS_A = ((0, 48, "p"), (48, 112, "q"), (160, 96, "q"))
CHUNKS_B = ((0, 96, "p"), (96, 80, "q"), (176, 80, "q"))
PR = 96
QR = 160
VMEM = 66_000_000
NT = (((1,), (1,)), ((), ()))
TN = (((0,), (0,)), ((), ()))


def dot(a, b, dims):
    return lax.dot_general(a, b, dims, preferred_element_type=F32)


def where_am_i():
    tp = lax.axis_index("tp")
    return tp // 8, (tp // 2) % 4, tp % 2


def tp_of(y, z, c):
    return y * 8 + z * 2 + c


def rdma(src, dst, ssem, rsem, dev):
    return pltpu.make_async_remote_copy(
        src_ref=src, dst_ref=dst, send_sem=ssem, recv_sem=rsem, device_id={"tp": dev}, device_id_type=MESH
    )


def greet(y, z, c):
    bar = pltpu.get_barrier_semaphore()

    def hello(dev):
        pl.semaphore_signal(bar, inc=1, device_id={"tp": dev}, device_id_type=MESH)

    hello(tp_of(y, z, 1 - c))
    hello(tp_of(1 - y, z, c))

    @pl.when(z > 0)
    def _():
        hello(tp_of(y, z - 1, c))

    @pl.when(z < 3)
    def _():
        hello(tp_of(y, z + 1, c))

    pl.semaphore_wait(bar, 2 + (z + 2) // 3 + (5 - z) // 3)


class Sends:
    def __init__(self):
        self.all = []

    def start(self, pred, make):
        self.all.append((pred, make))
        if pred is None:
            make().start()
        else:
            pl.when(pred)(lambda: make().start())

    def finish(self):
        for pred, make in self.all:
            if pred is None:
                make().wait_send()
            else:
                pl.when(pred)(lambda make=make: make().wait_send())


class Gather:
    def __init__(self, pos, own, full, rsem, zsem, ysem, sib_s, sib_r, chunks):
        self.y, self.z, self.c = pos
        self.own, self.full = own, full
        self.rsem, self.zsem, self.ysem, self.sib_s, self.sib_r = rsem, zsem, ysem, sib_s, sib_r
        self.chunks = chunks
        self.sends = Sends()

    def rows(self, y, z, k, c=None):
        r0, n = (0, SH) if k is None else self.chunks[k][:2]
        off = tp_of(y, z, self.c if c is None else c) * SH + r0
        return self.full.at[pl.ds(pl.multiple_of(off, 16), n)]

    def copy(self, dev, y, z, k, sems, own):
        r0, n, _ = self.chunks[k]
        src = self.own.at[pl.ds(r0, n)] if own else self.rows(y, z, k)
        d = y * 4 + z
        return rdma(src, self.rows(y, z, k), sems.at[d, k], self.rsem.at[d, k], dev)

    def send_z(self, step, y, z, k, pred=None, own=False):
        ok = self.z > 0 if step < 0 else self.z < 3
        if pred is not None:
            ok = jnp.logical_and(ok, pred)
        dev = tp_of(self.y, self.z + step, self.c)
        self.sends.start(ok, lambda: self.copy(dev, y, z, k, self.zsem.at[(step + 1) // 2], own))

    def send_y(self, y, z, k, pred=None, own=False):
        dev = tp_of(1 - self.y, self.z, self.c)
        self.sends.start(pred, lambda: self.copy(dev, y, z, k, self.ysem, own))

    def wait(self, y, z, k):
        self.copy(tp_of(1 - self.y, self.z, self.c), y, z, k, self.ysem, False).wait_recv()

    def sib_copy(self, y, z, c, own=False):
        d = y * 4 + z
        src = self.own if own else self.rows(y, z, None, c)
        return rdma(src, self.rows(y, z, None, c), self.sib_s.at[d], self.sib_r.at[d], tp_of(self.y, self.z, 1 - self.c))

    def send_sib(self, y, z, pred=None, own=False):
        self.sends.start(pred, lambda: self.sib_copy(y, z, self.c, own))

    def wait_sib(self, y, z):
        self.sib_copy(y, z, 1 - self.c).wait_recv()

    def begin(self):
        y, z = self.y, self.z
        for k, (_, _, kind) in enumerate(self.chunks):
            self.send_y(y, z, k, own=True)
            self.send_z(1, y, z, k, own=True)
            self.send_z(-1, y, z, k, own=True)
        self.send_sib(y, z, own=True)

    def turn(self):
        y, z = self.y, self.z
        for k, (_, _, kind) in enumerate(self.chunks):
            if kind == "p":
                self.wait(1 - y, z, k)
                self.send_z(1, 1 - y, z, k)
                self.send_z(-1, 1 - y, z, k)

    def step(self, s):
        y, z = self.y, self.z
        for k, (_, _, kind) in enumerate(self.chunks):
            for side in (-1, 1):
                zs = z + side * (s + 1)
                ok = zs >= 0 if side < 0 else zs <= 3
                for ys in (y, 1 - y) if kind == "p" else (y,):
                    pl.when(ok)(lambda ys=ys, zs=zs, k=k: self.wait(ys, zs, k))
                    if s < 2:
                        self.send_z(-side, ys, zs, k, pred=ok)
                if kind == "q":
                    self.send_y(y, zs, k, pred=ok)
        for side in (-1, 1):
            zs = z + side * (s + 1)
            self.send_sib(y, zs, pred=zs >= 0 if side < 0 else zs <= 3)

    def across(self, s):
        y, z = self.y, self.z
        for side in (-1, 1) if s else (0,):
            zs = z + side * s
            ok = None if s == 0 else zs >= 0 if side < 0 else zs <= 3

            def take(zs=zs):
                for k, (_, _, kind) in enumerate(self.chunks):
                    if kind == "q":
                        self.wait(1 - y, zs, k)

            if ok is None:
                take()
            else:
                pl.when(ok)(take)
            self.send_sib(1 - y, zs, pred=ok)


def local(src, dst, sem):
    return pltpu.make_async_copy(src, dst, sem)


def both(*copies):
    for cp in copies:
        cp.start()
    for cp in copies:
        cp.wait()


def kernel_a(dy, pre, w_down, w_in, full, hidden, dpre, dps, wis,
             wd_v, dy_v, pre_v, hid_v, dp_v, rsem, zsem, ysem, sib_s, sib_r, dps_s, dps_r, wis_sem, lsem):
    y, z, c = where_am_i()
    greet(y, z, c)
    g = Gather((y, z, c), dy, full, rsem, zsem, ysem, sib_s, sib_r, CHUNKS_A)
    g.begin()
    other = tp_of(y, z, 1 - c)
    w_copy = rdma(w_in, wis, wis_sem.at[0], wis_sem.at[1], other)
    w_copy.start()
    load_w = local(w_down, wd_v, lsem.at[4])
    load_w.start()

    def dps_copy(ys, zs):
        off = pl.multiple_of(tp_of(ys, zs, 1 - c) * SH, SH)
        d = ys * 4 + zs
        return rdma(dpre.at[pl.ds(off, SH)], dps.at[pl.ds(pl.multiple_of(d * SH, SH), SH)], dps_s.at[d], dps_r.at[d], other)

    def compute(ys, zs, cs):
        off = pl.multiple_of(tp_of(ys, zs, cs) * SH, SH)
        rows = pl.ds(off, SH)
        both(local(full.at[rows], dy_v, lsem.at[0]), local(pre.at[rows], pre_v, lsem.at[1]))

        def tile(j, _):
            cols = pl.ds(pl.multiple_of(j * 256, 256), 256)
            dh = dot(dy_v[...], wd_v[cols, :], NT)
            p = pre_v[:, cols].astype(F32)
            k = np.float32(np.sqrt(2 / np.pi))
            t = jnp.tanh(k * (p + 0.044715 * (p * p * p)))
            cdf = 0.5 * (1.0 + t)
            slope = cdf + 0.5 * p * (1.0 - t * t) * (k * (1.0 + 3 * 0.044715 * (p * p)))
            hid_v[:, cols] = (p * cdf).astype(BF16)
            dp_v[:, cols] = (dh * slope).astype(BF16)
            return 0

        lax.fori_loop(0, FL // 256, tile, 0)
        both(local(hid_v, hidden.at[rows], lsem.at[2]), local(dp_v, dpre.at[rows], lsem.at[3]))

    def shard(ys, zs, pred=None):
        def go():
            compute(ys, zs, c)
            g.wait_sib(ys, zs)
            compute(ys, zs, 1 - c)
            dps_copy(ys, zs).start()

        if pred is None:
            go()
        else:
            pl.when(pred)(go)

    both(local(dy, dy_v, lsem.at[0]))
    both(local(dy_v, g.rows(y, z, None), lsem.at[0]))
    load_w.wait()
    g.turn()

    def some(s):
        if s == 0:
            shard(y, z)
            g.step(0)
            g.across(0)
            shard(1 - y, z)
            return

        def one(i, _):
            side = 2 * (i // 2) - 1
            zs = z + side * s
            ys = jnp.where(i % 2 == 0, y, 1 - y)
            shard(ys, zs, jnp.logical_and(zs >= 0, zs <= 3))
            return 0

        lax.fori_loop(0, 4, one, 0)

    some(0)
    g.step(1)
    g.across(1)
    some(1)
    g.step(2)
    g.across(2)
    some(2)
    g.across(3)
    some(3)

    for d in range(8):
        cp = rdma(dpre.at[pl.ds(0, SH)], dps.at[pl.ds(d * SH, SH)], dps_s.at[d], dps_r.at[d], other)
        cp.wait_recv()
        cp.wait_send()
    w_copy.wait()
    g.sends.finish()


def kernel_b(x, dy, hidden, dpre, dps, w_in, wis,
             dx, dw_in, dw_down, full, pl_b, pr_b, ps_b, ql_b, qr_b, qs_b, qy_b, qys_b, py_b, pys_b,
             wo_v, ws_v, hid_v, acc, blk, xv, dpv, a1, a2, arr, obuf, tile_o, out_v,
             rsem, zsem, ysem, sib_s, sib_r, p_s, pl_r, pr_r, q_s, ql_r, qr_r, qy_s, qy_r, py_sem, lsem):
    y, z, c = where_am_i()
    greet(y, z, c)
    g = Gather((y, z, c), x, full, rsem, zsem, ysem, sib_s, sib_r, CHUNKS_B)
    g.begin()
    load_wo, load_ws, load_h = (
        local(w_in, wo_v, lsem.at[4]), local(wis, ws_v, lsem.at[5]), local(hidden, hid_v, lsem.at[6]))
    load_wo.start()
    load_ws.start()
    load_h.start()
    sends = Sends()
    left, right = tp_of(y, z - 1, c), tp_of(y, z + 1, c)
    over = tp_of(1 - y, z, c)
    inner = jnp.logical_and(z > 0, z < 3)
    high = z // 2
    far = high * z + (1 - high) * (3 - z)

    def target(i):
        o = (0, 1, 5 - far, far)[i]
        return high * o + (1 - high) * (3 - o)

    def term(ys, zs, r0, n):
        o = pl.multiple_of(tp_of(ys, zs, c) * SH + r0, 16)
        s = pl.multiple_of((ys * 4 + zs) * SH + r0, 16)
        both(local(dpre.at[pl.ds(o, n)], a1.at[pl.ds(0, n)], lsem.at[0]),
             local(dps.at[pl.ds(s, n)], a2.at[pl.ds(0, n)], lsem.at[1]))

        def tile(j, _):
            cols = pl.ds(pl.multiple_of(j * 512, 512), 512)
            blk[0:n, cols] = dot(a1[0:n, :], wo_v[cols, :], NT) + dot(a2[0:n, :], ws_v[cols, :], NT)
            return 0

        lax.fori_loop(0, D // 512, tile, 0)

    def add(buf, wait, n):
        wait()
        both(local(buf, arr.at[pl.ds(0, n)], lsem.at[2]))

        def tile(j, _):
            cols = pl.ds(pl.multiple_of(j * 512, 512), 512)
            blk[0:n, cols] += arr[0:n, cols].astype(F32)
            return 0

        lax.fori_loop(0, D // 512, tile, 0)

    def store(buf, n):
        def tile(j, _):
            cols = pl.ds(pl.multiple_of(j * 512, 512), 512)
            obuf[0:n, cols] = blk[0:n, cols].astype(BF16)
            return 0

        lax.fori_loop(0, D // 512, tile, 0)
        both(local(obuf.at[pl.ds(0, n)], buf, lsem.at[3]))

    def p_copy(ys, v, dev, rightward):
        i = ys * 4 + v
        dst, sem = (pl_b, pl_r) if rightward else (pr_b, pr_r)
        return rdma(ps_b.at[i], dst.at[i], p_s.at[i], sem.at[i], dev)

    def q_copy(v, dev, rightward):
        dst, sem = (ql_b, ql_r) if rightward else (qr_b, qr_r)
        return rdma(qs_b.at[v], dst.at[v], q_s.at[v], sem.at[v], dev)

    def qy_copy(v):
        return rdma(qys_b.at[v], qy_b.at[v], qy_s.at[v], qy_r.at[v], over)

    def py_copy():
        return rdma(pys_b, py_b, py_sem.at[0], py_sem.at[1], over)

    def p_line(i, pred):
        v = target(i)
        up, down = v > z, v < z

        def go():
            for ys in (1 - y, y):
                term(ys, v, 0, PR)
                pl.when(jnp.logical_and(inner, up))(
                    lambda: add(pl_b.at[ys * 4 + v], lambda: p_copy(ys, v, right, True).wait_recv(), PR))
                pl.when(jnp.logical_and(inner, down))(
                    lambda: add(pr_b.at[ys * 4 + v], lambda: p_copy(ys, v, left, False).wait_recv(), PR))
                store(ps_b.at[ys * 4 + v], PR)
                pl.when(up)(lambda: p_copy(ys, v, right, True).start())
                pl.when(down)(lambda: p_copy(ys, v, left, False).start())

        pl.when(pred)(go)

    def q_line(i, pred):
        v = target(i)
        up, down = v > z, v < z

        def go():
            term(y, v, PR, QR)
            add(qy_b.at[v], lambda: qy_copy(v).wait_recv(), QR)
            pl.when(jnp.logical_and(inner, up))(lambda: add(ql_b.at[v], lambda: q_copy(v, right, True).wait_recv(), QR))
            pl.when(jnp.logical_and(inner, down))(lambda: add(qr_b.at[v], lambda: q_copy(v, left, False).wait_recv(), QR))
            store(qs_b.at[v], QR)
            pl.when(up)(lambda: q_copy(v, right, True).start())
            pl.when(down)(lambda: q_copy(v, left, False).start())

        pl.when(pred)(go)

    def towards(i, pred):
        p_line(i, pred)
        q_line(i, pred)

    def p_last(ys):
        term(ys, z, 0, PR)
        i = ys * 4 + z
        pl.when(z > 0)(lambda: add(pl_b.at[i], lambda: p_copy(ys, z, right, True).wait_recv(), PR))
        pl.when(z < 3)(lambda: add(pr_b.at[i], lambda: p_copy(ys, z, left, False).wait_recv(), PR))

    def q_last():
        term(y, z, PR, QR)
        add(qy_b.at[z], lambda: qy_copy(z).wait_recv(), QR)
        pl.when(z > 0)(lambda: add(ql_b.at[z], lambda: q_copy(z, right, True).wait_recv(), QR))
        pl.when(z < 3)(lambda: add(qr_b.at[z], lambda: q_copy(z, left, False).wait_recv(), QR))
        store(dx.at[pl.ds(PR, QR)], QR)

    def down_tiles(first, count):
        def one(j, _):
            cols = pl.ds(pl.multiple_of(j * 512, 512), 512)
            both(local(dy.at[:, cols], tile_o, lsem.at[0]))

            def row(m, _):
                ms = pl.ds(pl.multiple_of(m * 256, 256), 256)
                out_v[ms, :] = dot(hid_v[:, ms], tile_o[...], TN).astype(BF16)
                return 0

            lax.fori_loop(0, FL // 256, row, 0)
            both(local(out_v, dw_down.at[:, cols], lsem.at[0]))
            return 0

        lax.fori_loop(first, first + count, one, 0)

    def in_step(ys, zs):
        rows = pl.ds(pl.multiple_of(tp_of(ys, zs, 0) * SH, SH), 2 * SH)
        both(local(full.at[rows], xv, lsem.at[0]), local(dpre.at[rows], dpv, lsem.at[1]))

        def row(m, _):
            ms = pl.ds(pl.multiple_of(m * 256, 256), 256)
            acc[ms, :] += dot(xv[:, ms], dpv[...], TN)
            return 0

        lax.fori_loop(0, D // 256, row, 0)

    def ready(s):
        def one(i, _):
            side = 2 * (i // 2) - 1
            zs = z + side * s
            ys = jnp.where(i % 2 == 0, y, 1 - y)

            @pl.when(jnp.logical_and(zs >= 0, zs <= 3))
            def _():
                g.wait_sib(ys, zs)
                in_step(ys, zs)

            return 0

        lax.fori_loop(2 if s == 0 else 0, 4, one, 0)

    load_wo.wait()
    load_ws.wait()
    for i in range(4):
        v = target(i)
        term(1 - y, v, PR, QR)
        store(qys_b.at[v], QR)
        qy_copy(v).start()
    g.turn()
    both(local(x, obuf_rows(xv), lsem.at[0]))
    both(local(obuf_rows(xv), g.rows(y, z, None), lsem.at[0]))

    def zero(m, _):
        acc[pl.ds(pl.multiple_of(m * 256, 256), 256), :] = jnp.zeros((256, FL), F32)
        return 0

    lax.fori_loop(0, D // 256, zero, 0)
    load_h.wait()
    outer = jnp.logical_not(inner)
    towards(0, outer)
    down_tiles(0, 2)
    g.step(0)
    g.across(0)
    towards(0, inner)
    ready(0)
    down_tiles(2, 2)
    towards(1, outer)
    g.step(1)
    towards(1, inner)
    g.across(1)
    down_tiles(4, 4)
    towards(2, outer)
    g.step(2)
    towards(2, inner)
    ready(1)
    g.across(2)
    ready(2)
    p_last(1 - y)
    store(pys_b, PR)
    py_copy().start()
    q_last()
    p_last(y)
    add(py_b, lambda: py_copy().wait_recv(), PR)
    store(dx.at[pl.ds(0, PR)], PR)
    g.across(3)
    ready(3)

    def out(m, _):
        ms = pl.ds(pl.multiple_of(m * 512, 512), 512)
        dpv[...] = acc[ms, :].astype(BF16)
        both(local(dpv, dw_in.at[ms], lsem.at[0]))
        return 0

    lax.fori_loop(0, D // 512, out, 0)

    for i in range(3):
        v = target(i)
        for ys in (1 - y, y):
            p_copy(ys, v, left, False).wait_send()
        q_copy(v, left, False).wait_send()
    for i in range(4):
        qy_copy(target(i)).wait_send()
    py_copy().wait_send()
    g.sends.finish()


def obuf_rows(xv):
    return xv.at[pl.ds(0, SH)]


def solution(mesh):
    any_ = pl.BlockSpec(memory_space=pl.ANY)
    dma = pltpu.SemaphoreType.DMA

    def arr(*shape):
        return jax.ShapeDtypeStruct(shape, BF16)

    gather_sems = [dma((8, 3)), dma((2, 8, 3)), dma((8, 3)), dma((8,)), dma((8,))]

    def step(x, dy, pre, w_in, w_down):
        full, hidden, dpre, dps, wis = pl.pallas_call(
            kernel_a,
            name="gather_dy",
            out_shape=[arr(D, D), arr(D, FL), arr(D, FL), arr(8 * SH, FL), arr(D, FL)],
            in_specs=[any_] * 4,
            out_specs=[any_] * 5,
            scratch_shapes=[
                pltpu.VMEM((FL, D), BF16), pltpu.VMEM((SH, D), BF16), pltpu.VMEM((SH, FL), BF16),
                pltpu.VMEM((SH, FL), BF16), pltpu.VMEM((SH, FL), BF16),
                *gather_sems, dma((8,)), dma((8,)), dma((2,)), dma((5,)),
            ],
            compiler_params=pltpu.CompilerParams(collective_id=0, has_side_effects=True, vmem_limit_bytes=VMEM),
        )(dy, pre, w_down, w_in)
        out = pl.pallas_call(
            kernel_b,
            name="reduce_dx",
            out_shape=[
                arr(SH, D), arr(D, FL), arr(FL, D), arr(D, D),
                arr(8, PR, D), arr(8, PR, D), arr(8, PR, D),
                arr(4, QR, D), arr(4, QR, D), arr(4, QR, D), arr(4, QR, D), arr(4, QR, D),
                arr(PR, D), arr(PR, D),
            ],
            in_specs=[any_] * 7,
            out_specs=[any_] * 14,
            scratch_shapes=[
                pltpu.VMEM((D, FL), BF16), pltpu.VMEM((D, FL), BF16), pltpu.VMEM((D, FL), BF16),
                pltpu.VMEM((D, FL), F32), pltpu.VMEM((QR, D), F32), pltpu.VMEM((2 * SH, D), BF16),
                pltpu.VMEM((2 * SH, FL), BF16), pltpu.VMEM((QR, FL), BF16), pltpu.VMEM((QR, FL), BF16),
                pltpu.VMEM((QR, D), BF16), pltpu.VMEM((QR, D), BF16), pltpu.VMEM((D, 512), BF16), pltpu.VMEM((FL, 512), BF16),
                *gather_sems,
                dma((8,)), dma((8,)), dma((8,)), dma((4,)), dma((4,)), dma((4,)), dma((4,)), dma((4,)), dma((2,)), dma((7,)),
            ],
            compiler_params=pltpu.CompilerParams(collective_id=1, has_side_effects=True, vmem_limit_bytes=VMEM),
        )(x, full, hidden, dpre, dps, w_in, wis)
        return out[0], out[1], out[2]

    rows = P(("dp", "tp"), None)
    cols = P("dp", "tp")
    return jax.shard_map(
        step, mesh=mesh,
        in_specs=(rows, rows, cols, P(None, "tp"), P("tp", None)),
        out_specs=(rows, cols, rows),
        check_vma=False,
    )
```

time: 1360 us -> 625 us (0.46)
  the two profiles are of different devices: /device:TPU:0 before, /device:TPU:10 now
where the time goes in v1:
time: 625 us; the launch traced here: 623 us
  Pallas kernels  604 us (97%)
  local copies, waits for them, and re-layouts  18.8 us (3%)
    pallas_call x1, Pallas kernels, step(): pl.pallas_call(kernel_b, name='reduce_dx', out_shape=[arr(SH, D), arr(D,...  398 us
    pallas_call x1, Pallas kernels, step(): pl.pallas_call(kernel_a, name='gather_dy', out_shape=[arr(D, D), arr(D, F...  206 us
    unnamed x3, local copies, waits for them, and re-layouts  18.8 us

profile of v1, /device:TPU:10, one launch (start us, length us, event | category | flops | bytes accessed | tf_op | source)
XLA Modules:
  0.0 623.1 jit_solution(16860070971018438163)
XLA Ops:
  0.6 205.7 %gather_dy.1 = (bf16[4096,4096]{1,0:T(8,128)(2,1)}, bf16[4096,1024]{1,0:T(8,128)(2,1)}, bf16[4096,1024]{1,0:T(8,128)(2,1)}, bf16[2048,1024]{1,0:T(8,128)(2,1)}, bf16[4096,1024]{1,0:T(8,128)(2,1)}) custom-call(bf16[256,4096]{1,0:T(8,128)(2,1)} %dy.1, bf16[4096,1024]{1,0:T(8,128)(2,1)} %pre.1, bf16[1024,4096]{1,0:T(8,128)(2,1)} %w_down.1, bf16[4096,1024]{1,0:T(8,128)(2,1)} %w_in.3), custom_call_target="tpu_custom_call" | custom-call | tf_op jit(solution)/shard_map/gather_dy/pallas_call | solution.py:519
  206.3 398.0 %reduce_dx.1 = (bf16[256,4096]{1,0:T(8,128)(2,1)}, bf16[4096,1024]{1,0:T(8,128)(2,1)}, bf16[1024,4096]{1,0:T(8,128)(2,1)}, bf16[4096,4096]{1,0:T(8,128)(2,1)}, b...) custom-call(bf16[256,4096]{1,0:T(8,128)(2,1)} %x.1, ...), custom_call_target="tpu_custom_call" | custom-call | tf_op jit(solution)/shard_map/reduce_dx/pallas_call | solution.py:532
  604.4 3.1 copy.11
  607.5 7.8 %copy.12 = bf16[4096,1024]{1,0:T(8,128)(2,1)} copy(bf16[4096,1024]{1,0:T(8,128)(2,1)} %get-tuple-element.23) | data formatting | bytes 16777216
  615.2 7.9 %copy.13 = bf16[1024,4096]{1,0:T(8,128)(2,1)} copy(bf16[1024,4096]{1,0:T(8,128)(2,1)} %get-tuple-element.24) | data formatting | bytes 16777216

commit v2 on v0

v2 whole, which is shorter than its diff:
```python
import functools

import jax
import jax.numpy as jnp
import numpy as np
from jax import lax
from jax.experimental import pallas as pl
from jax.experimental.pallas import tpu as pltpu
from jax.sharding import PartitionSpec as P

MESH = pl.DeviceIdType.MESH
F32, BF16 = jnp.float32, jnp.bfloat16
D = 4096
FL = 1024
SH = 256
CHUNKS_A = ((0, 128, "q"), (128, 128, "q"))
CHUNKS_B = ((0, 112, "p"), (112, 80, "q"), (192, 64, "q"))
PR = 80
QR = 176
VMEM = 66_000_000
NT = (((1,), (1,)), ((), ()))
TN = (((0,), (0,)), ((), ()))


def dot(a, b, dims):
    return lax.dot_general(a, b, dims, preferred_element_type=F32)


def where_am_i():
    tp = lax.axis_index("tp")
    return tp // 8, (tp // 2) % 4, tp % 2


def tp_of(y, z, c):
    return y * 8 + z * 2 + c


def rdma(src, dst, ssem, rsem, dev):
    return pltpu.make_async_remote_copy(
        src_ref=src, dst_ref=dst, send_sem=ssem, recv_sem=rsem, device_id={"tp": dev}, device_id_type=MESH
    )


def greet(y, z, c):
    bar = pltpu.get_barrier_semaphore()

    def hello(dev):
        pl.semaphore_signal(bar, inc=1, device_id={"tp": dev}, device_id_type=MESH)

    hello(tp_of(y, z, 1 - c))
    hello(tp_of(1 - y, z, c))

    @pl.when(z > 0)
    def _():
        hello(tp_of(y, z - 1, c))

    @pl.when(z < 3)
    def _():
        hello(tp_of(y, z + 1, c))

    pl.semaphore_wait(bar, 2 + (z + 2) // 3 + (5 - z) // 3)


class Sends:
    def __init__(self):
        self.all = []

    def start(self, pred, make):
        self.all.append((pred, make))
        if pred is None:
            make().start()
        else:
            pl.when(pred)(lambda: make().start())

    def finish(self):
        for pred, make in self.all:
            if pred is None:
                make().wait_send()
            else:
                pl.when(pred)(lambda make=make: make().wait_send())


class Gather:
    def __init__(self, pos, own, full, rsem, zsem, ysem, sib_s, sib_r, chunks):
        self.y, self.z, self.c = pos
        self.own, self.full = own, full
        self.rsem, self.zsem, self.ysem, self.sib_s, self.sib_r = rsem, zsem, ysem, sib_s, sib_r
        self.chunks = chunks
        self.sends = Sends()

    def rows(self, y, z, k, c=None):
        r0, n = (0, SH) if k is None else self.chunks[k][:2]
        off = tp_of(y, z, self.c if c is None else c) * SH + r0
        return self.full.at[pl.ds(pl.multiple_of(off, 16), n)]

    def copy(self, dev, y, z, k, sems, own):
        r0, n, _ = self.chunks[k]
        src = self.own.at[pl.ds(r0, n)] if own else self.rows(y, z, k)
        d = y * 4 + z
        return rdma(src, self.rows(y, z, k), sems.at[d, k], self.rsem.at[d, k], dev)

    def send_z(self, step, y, z, k, pred=None, own=False):
        ok = self.z > 0 if step < 0 else self.z < 3
        if pred is not None:
            ok = jnp.logical_and(ok, pred)
        dev = tp_of(self.y, self.z + step, self.c)
        self.sends.start(ok, lambda: self.copy(dev, y, z, k, self.zsem.at[(step + 1) // 2], own))

    def send_y(self, y, z, k, pred=None, own=False):
        dev = tp_of(1 - self.y, self.z, self.c)
        self.sends.start(pred, lambda: self.copy(dev, y, z, k, self.ysem, own))

    def wait(self, y, z, k):
        self.copy(tp_of(1 - self.y, self.z, self.c), y, z, k, self.ysem, False).wait_recv()

    def sib_copy(self, y, z, c, own=False):
        d = y * 4 + z
        src = self.own if own else self.rows(y, z, None, c)
        return rdma(src, self.rows(y, z, None, c), self.sib_s.at[d], self.sib_r.at[d], tp_of(self.y, self.z, 1 - self.c))

    def send_sib(self, y, z, pred=None, own=False):
        self.sends.start(pred, lambda: self.sib_copy(y, z, self.c, own))

    def wait_sib(self, y, z):
        self.sib_copy(y, z, 1 - self.c).wait_recv()

    def begin_y(self):
        for k in range(len(self.chunks)):
            self.send_y(self.y, self.z, k, own=True)
        self.send_sib(self.y, self.z, own=True)

    def begin_z(self):
        for k in range(len(self.chunks)):
            self.send_z(1, self.y, self.z, k, own=True)
            self.send_z(-1, self.y, self.z, k, own=True)

    def turn(self):
        y, z = self.y, self.z
        for k, (_, _, kind) in enumerate(self.chunks):
            if kind == "p":
                self.wait(1 - y, z, k)
                self.send_z(1, 1 - y, z, k)
                self.send_z(-1, 1 - y, z, k)

    def step(self, s):
        y, z = self.y, self.z
        for k, (_, _, kind) in enumerate(self.chunks):
            for side in (-1, 1):
                zs = z + side * (s + 1)
                ok = zs >= 0 if side < 0 else zs <= 3
                for ys in (y, 1 - y) if kind == "p" else (y,):
                    pl.when(ok)(lambda ys=ys, zs=zs, k=k: self.wait(ys, zs, k))
                    if s < 2:
                        self.send_z(-side, ys, zs, k, pred=ok)
                if kind == "q":
                    self.send_y(y, zs, k, pred=ok)
        for side in (-1, 1):
            zs = z + side * (s + 1)
            self.send_sib(y, zs, pred=zs >= 0 if side < 0 else zs <= 3)

    def across(self, s):
        y, z = self.y, self.z
        for side in (-1, 1) if s else (0,):
            zs = z + side * s
            ok = None if s == 0 else zs >= 0 if side < 0 else zs <= 3

            def take(zs=zs):
                for k, (_, _, kind) in enumerate(self.chunks):
                    if kind == "q":
                        self.wait(1 - y, zs, k)

            if ok is None:
                take()
            else:
                pl.when(ok)(take)
            self.send_sib(1 - y, zs, pred=ok)


def local(src, dst, sem):
    return pltpu.make_async_copy(src, dst, sem)


def both(*copies):
    for cp in copies:
        cp.start()
    for cp in copies:
        cp.wait()


def kernel(x, dy, pre, w_in, w_down,
           dx, acc_o, dw_down, fy, fx, hidden, dpre, dps, wis, pl_b, pr_b, ps_b, ql_b, qr_b, qs_b, qy_b, qys_b, py_b, pys_b,
           wd_v, wo_v, ws_v, acc, big, blk, a1, a2, arr, obuf, pre_v, hid_v, dp_v,
           y_rs, y_zs, y_ys, y_ss, y_sr, x_rs, x_zs, x_ys, x_ss, x_sr,
           dps_s, dps_r, wis_sem, p_s, pl_r, pr_r, q_s, ql_r, qr_r, qy_s, qy_r, py_sem, lsem):
    y, z, c = where_am_i()
    greet(y, z, c)
    gy = Gather((y, z, c), dy, fy, y_rs, y_zs, y_ys, y_ss, y_sr, CHUNKS_A)
    gx = Gather((y, z, c), x, fx, x_rs, x_zs, x_ys, x_ss, x_sr, CHUNKS_B)
    gy.begin_y()
    gy.begin_z()
    other = tp_of(y, z, 1 - c)
    left, right, over = tp_of(y, z - 1, c), tp_of(y, z + 1, c), tp_of(1 - y, z, c)
    w_copy = rdma(w_in, wis, wis_sem.at[0], wis_sem.at[1], other)
    w_copy.start()
    load_w = local(w_down, wd_v, lsem.at[4])
    load_wo = local(w_in, wo_v, lsem.at[5])
    load_ws = local(wis, ws_v, lsem.at[6])
    load_w.start()
    load_wo.start()
    xv = big.at[pl.ds(0, 2 * SH)]

    def place_own(src, g):
        via = big.at[pl.ds(0, SH)]
        both(local(src, via, lsem.at[0]))
        both(local(via, g.rows(y, z, None), lsem.at[0]))

    def clear():
        def zero(m, _):
            acc[m // 4, pl.ds(pl.multiple_of((m % 4) * 256, 256), 256), :] = jnp.zeros((256, FL), F32)
            return 0

        lax.fori_loop(0, 16, zero, 0)

    def dps_copy(ys, zs):
        off = pl.multiple_of(tp_of(ys, zs, 1 - c) * SH, SH)
        d = ys * 4 + zs
        return rdma(dpre.at[pl.ds(off, SH)], dps.at[pl.ds(pl.multiple_of(d * SH, SH), SH)], dps_s.at[d], dps_r.at[d], other)


    def weigh():
        def weight(j, _):
            ms = pl.ds(pl.multiple_of((j % 4) * 256, 256), 256)
            cols = pl.ds(pl.multiple_of((j // 4) * FL, FL), FL)
            acc[j // 4, ms, :] += dot(hid_v[:, ms], big[0:512, cols], TN)
            return 0

        lax.fori_loop(0, 16, weight, 0)

    def chip_rows(ys, zs):
        return pl.ds(pl.multiple_of(tp_of(ys, zs, 0) * SH, SH), 2 * SH)

    def pair(ys, zs, pred=None, now=True):
        def go():
            gy.wait_sib(ys, zs)
            rows = chip_rows(ys, zs)
            both(local(fy.at[rows], xv, lsem.at[0]), local(pre.at[rows], pre_v, lsem.at[1]))

            def tile(j, _):
                cols = pl.ds(pl.multiple_of(j * 256, 256), 256)
                dh = dot(big[0:512, :], wd_v[cols, :], NT)
                p = pre_v[:, cols].astype(F32)
                k = np.float32(np.sqrt(2 / np.pi))
                t = jnp.tanh(k * (p + 0.044715 * (p * p * p)))
                cdf = 0.5 * (1.0 + t)
                slope = cdf + 0.5 * p * (1.0 - t * t) * (k * (1.0 + 3 * 0.044715 * (p * p)))
                hid_v[:, cols] = (p * cdf).astype(BF16)
                dp_v[:, cols] = (dh * slope).astype(BF16)
                return 0

            lax.fori_loop(0, FL // 256, tile, 0)
            out = local(dp_v, dpre.at[rows], lsem.at[3])
            if now:
                out.start()
                weigh()
                out.wait()
            else:
                both(out, local(hid_v, hidden.at[rows], lsem.at[2]))
            dps_copy(ys, zs).start()

        if pred is None:
            go()
        else:
            pl.when(pred)(go)

    def early(ys, zs, pred):
        pair(ys, zs, pred, now=False)

    def late(ys, zs):
        rows = chip_rows(ys, zs)
        both(local(fy.at[rows], xv, lsem.at[0]), local(hidden.at[rows], hid_v, lsem.at[1]))
        weigh()

    def pairs(do, s, flip):
        def one(i, _):
            zs = z + (2 * i - 1) * s
            do(1 - y if flip else y, zs, jnp.logical_and(zs >= 0, zs <= 3))
            return 0

        lax.fori_loop(0, 2, one, 0)

    place_own(dy, gy)
    clear()
    load_w.wait()
    gy.turn()
    pair(y, z)
    gy.step(0)
    gy.across(0)
    pair(1 - y, z)
    pairs(pair, 1, False)
    gy.step(1)
    gx.begin_z()
    gy.across(1)
    pairs(early, 1, True)
    gy.step(2)
    gx.begin_y()
    pairs(early, 2, False)
    gy.across(2)
    pairs(early, 2, True)
    pairs(early, 3, False)
    w_copy.wait()
    load_ws.start()
    gy.across(3)
    pairs(early, 3, True)


    inner = jnp.logical_and(z > 0, z < 3)
    outer = jnp.logical_not(inner)
    high = z // 2
    inward = 1 - 2 * high
    far = high * z + (1 - high) * (3 - z)

    def target(i):
        o = (0, 1, 5 - far, far)[i]
        return high * o + (1 - high) * (3 - o)

    def fetch(ys, zs, r0, n, at):
        o = pl.multiple_of(tp_of(ys, zs, c) * SH + r0, 16)
        s = pl.multiple_of((ys * 4 + zs) * SH + r0, 16)
        return (local(dpre.at[pl.ds(o, n)], a1.at[pl.ds(at, n)], lsem.at[0]),
                local(dps.at[pl.ds(s, n)], a2.at[pl.ds(at, n)], lsem.at[1]))

    def fetch_all(parts):
        for part in parts:
            both(*part)

    def cols512(j):
        return pl.ds(pl.multiple_of(j * 512, 512), 512)

    def q_terms():
        fetch_all([fetch(1 - y, target(i), PR, QR, i * QR) for i in range(4)])

        def tile(j, _):
            cols = cols512(j)
            big[:, cols] = (dot(a1[...], wo_v[cols, :], NT) + dot(a2[...], ws_v[cols, :], NT)).astype(BF16)
            return 0

        lax.fori_loop(0, D // 512, tile, 0)
        both(*(local(big.at[pl.ds(i * QR, QR)], qys_b.at[target(i)], lsem.at[i]) for i in range(4)))

    def terms(v):
        fetch_all([fetch(1 - y, v, 0, PR, 0), fetch(y, v, 0, SH, PR)])
        n = PR + SH

        def tile(j, _):
            cols = cols512(j)
            blk[:, cols] = dot(a1[0:n, :], wo_v[cols, :], NT) + dot(a2[0:n, :], ws_v[cols, :], NT)
            return 0

        lax.fori_loop(0, D // 512, tile, 0)

    def add(buf, copy, at, n):
        copy.wait_recv()
        both(local(buf, arr.at[pl.ds(0, n)], lsem.at[2]))

        def tile(j, _):
            cols = cols512(j)
            blk[at:at + n, cols] += arr[0:n, cols].astype(F32)
            return 0

        lax.fori_loop(0, D // 512, tile, 0)

    def store(buf, at, n):
        def tile(j, _):
            cols = cols512(j)
            obuf[0:n, cols] = blk[at:at + n, cols].astype(BF16)
            return 0

        lax.fori_loop(0, D // 512, tile, 0)
        both(local(obuf.at[pl.ds(0, n)], buf, lsem.at[3]))

    def p_copy(ys, v, dev, rightward):
        i = ys * 4 + v
        dst, sem = (pl_b, pl_r) if rightward else (pr_b, pr_r)
        return rdma(ps_b.at[i], dst.at[i], p_s.at[i], sem.at[i], dev)

    def q_copy(v, dev, rightward):
        dst, sem = (ql_b, ql_r) if rightward else (qr_b, qr_r)
        return rdma(qs_b.at[v], dst.at[v], q_s.at[v], sem.at[v], dev)

    def qy_copy(v):
        return rdma(qys_b.at[v], qy_b.at[v], qy_s.at[v], qy_r.at[v], over)

    def py_copy():
        return rdma(pys_b, py_b, py_sem.at[0], py_sem.at[1], over)

    def from_left(ok, ys, v, at):
        if ys is None:
            pl.when(ok)(lambda: add(ql_b.at[v], q_copy(v, right, True), at, QR))
        else:
            pl.when(ok)(lambda: add(pl_b.at[ys * 4 + v], p_copy(ys, v, right, True), at, PR))

    def from_right(ok, ys, v, at):
        if ys is None:
            pl.when(ok)(lambda: add(qr_b.at[v], q_copy(v, left, False), at, QR))
        else:
            pl.when(ok)(lambda: add(pr_b.at[ys * 4 + v], p_copy(ys, v, left, False), at, PR))

    def towards(i, pred, fill=(None, None)):
        v = target(i)
        up, down = v > z, v < z

        def go():
            terms(v)
            for ys, at, other_work in ((1 - y, 0, fill[0]), (y, PR, fill[1])):
                from_left(jnp.logical_and(inner, up), ys, v, at)
                from_right(jnp.logical_and(inner, down), ys, v, at)
                store(ps_b.at[ys * 4 + v], at, PR)
                pl.when(up)(lambda ys=ys: p_copy(ys, v, right, True).start())
                pl.when(down)(lambda ys=ys: p_copy(ys, v, left, False).start())
                if other_work is not None:
                    other_work()
            add(qy_b.at[v], qy_copy(v), 2 * PR, QR)
            from_left(jnp.logical_and(inner, up), None, v, 2 * PR)
            from_right(jnp.logical_and(inner, down), None, v, 2 * PR)
            store(qs_b.at[v], 2 * PR, QR)
            pl.when(up)(lambda: q_copy(v, right, True).start())
            pl.when(down)(lambda: q_copy(v, left, False).start())

        pl.when(pred)(go)

    def arrived(ys, at):
        from_left(z > 0, ys, z, at)
        from_right(z < 3, ys, z, at)

    def in_step(ys, zs, pred=None):
        def go():
            gx.wait_sib(ys, zs)
            rows = chip_rows(ys, zs)
            both(local(fx.at[rows], xv, lsem.at[0]), local(dpre.at[rows], dp_v, lsem.at[1]))

            def row(m, _):
                here = pl.ds(pl.multiple_of((m % 4) * 256, 256), 256)
                acc[m // 4, here, :] += dot(big[0:512, pl.ds(pl.multiple_of(m * 256, 256), 256)], dp_v[...], TN)
                return 0

            lax.fori_loop(0, D // 256, row, 0)

        if pred is None:
            go()
        else:
            pl.when(pred)(go)

    def write(to):
        def one(m, _):
            h0, h1 = pl.ds(0, 512), pl.ds(512, 512)
            hid_v[...] = acc[m, h0, :].astype(BF16)
            first = local(hid_v, to(m, 0), lsem.at[0])
            first.start()
            pre_v[...] = acc[m, h1, :].astype(BF16)
            both(local(pre_v, to(m, 1), lsem.at[1]))
            first.wait()
            return 0

        lax.fori_loop(0, 4, one, 0)

    for d in range(8):
        cp = rdma(dpre.at[pl.ds(0, SH)], dps.at[pl.ds(d * SH, SH)], dps_s.at[d], dps_r.at[d], other)
        cp.wait_recv()
        cp.wait_send()
    load_wo.wait()
    load_ws.wait()
    q_terms()
    qy_copy(target(0)).start()
    qy_copy(target(1)).start()
    gx.turn()
    place_own(x, gx)
    towards(0, outer)

    def late_first(k, _):
        late(jnp.where(inner, 1 - y, jnp.where(k == 0, 1 - y, y)), z + inward * jnp.where(inner, 1 - 2 * k, 1 + k))
        return 0

    def late_rest(k, _):
        late(jnp.where(k % 2 == 0, 1 - y, y), z + inward * (1 + (k + 1) // 2))
        return 0

    lax.fori_loop(0, 2, late_first, 0)
    gx.step(0)
    gx.across(0)
    qy_copy(target(2)).start()
    towards(0, inner, (lambda: late(y, z + 2 * inward), lambda: late(1 - y, z + 2 * inward)))
    towards(1, outer)
    gx.step(1)
    qy_copy(target(3)).start()
    lax.fori_loop(2, jnp.where(inner, 2, 5), late_rest, 0)
    write(lambda m, h: dw_down.at[pl.ds(h * 512, 512), pl.ds(pl.multiple_of(m * FL, FL), FL)])
    clear()
    in_step(y, z)
    in_step(1 - y, z, outer)
    towards(1, inner, (lambda: in_step(1 - y, z), lambda: in_step(y, z - 1)))
    towards(2, outer)
    gx.across(1)
    gx.step(2)
    towards(2, inner)
    in_step(y, jnp.where(inner, z + 1, z + inward))
    pairs(in_step, 1, True)
    gx.across(2)
    in_step(y, z + 2 * inward, outer)
    in_step(1 - y, z + 2 * inward, outer)
    save = local(acc, acc_o, lsem.at[4])
    save.start()
    terms(z)
    arrived(1 - y, 0)
    store(pys_b, 0, PR)
    py_copy().start()
    add(qy_b.at[z], qy_copy(z), 2 * PR, QR)
    arrived(None, 2 * PR)
    store(dx.at[pl.ds(PR, QR)], 2 * PR, QR)
    arrived(y, PR)
    add(py_b, py_copy(), PR, PR)
    store(dx.at[pl.ds(0, PR)], PR, PR)
    gx.across(3)
    gx.wait_sib(y, 3 - 3 * high)
    gx.wait_sib(1 - y, 3 - 3 * high)
    save.wait()

    for i in range(3):
        v = target(i)
        for ys in (1 - y, y):
            p_copy(ys, v, left, False).wait_send()
        q_copy(v, left, False).wait_send()
    for i in range(4):
        qy_copy(target(i)).wait_send()
    py_copy().wait_send()
    gy.sends.finish()
    gx.sends.finish()


def place(acc, x0, x1, dp0, dp1, down_in, dx_in, dw_in, down, dx):
    total = acc[...] + dot(x0[...], dp0[...], TN) + dot(x1[...], dp1[...], TN)
    dw_in[...] = total.astype(BF16)
    down[...] = down_in[...]
    dx[...] = dx_in[...]


def finish(acc, full, dpre, down, dx):
    def chip(other):
        tp = lax.axis_index("tp")
        y = tp // 8
        return (1 - y if other else y) * 4 + 3 - 3 * ((tp // 2) % 4 // 2)

    steps = 8
    tall = pl.BlockSpec((FL // steps, D), lambda i: (i, 0))
    flat = pl.BlockSpec((SH // steps, D), lambda i: (i, 0))
    part = pl.BlockSpec((D // steps, FL), lambda i: (i, 0))
    return pl.pallas_call(
        place,
        name="finish",
        grid=(steps,),
        in_specs=[
            part,
            pl.BlockSpec((2 * SH, D // steps), lambda i: (chip(False), i)),
            pl.BlockSpec((2 * SH, D // steps), lambda i: (chip(True), i)),
            pl.BlockSpec((2 * SH, FL), lambda i: (chip(False), 0)),
            pl.BlockSpec((2 * SH, FL), lambda i: (chip(True), 0)),
            tall, flat,
        ],
        out_specs=[part, tall, flat],
        out_shape=[jax.ShapeDtypeStruct(s, BF16) for s in ((D, FL), (FL, D), (SH, D))],
        compiler_params=pltpu.CompilerParams(vmem_limit_bytes=48_000_000),
    )(acc.reshape(D, FL), full, full, dpre, dpre, down, dx)


def solution(mesh):
    any_ = pl.BlockSpec(memory_space=pl.ANY)
    dma = pltpu.SemaphoreType.DMA

    def arr(*shape):
        return jax.ShapeDtypeStruct(shape, BF16)

    def vmem(*shape, dtype=BF16):
        return pltpu.VMEM(shape, dtype)

    gather_sems = [dma((8, 3)), dma((2, 8, 3)), dma((8, 3)), dma((8,)), dma((8,))]

    def step(x, dy, pre, w_in, w_down):
        outs = [
            arr(SH, D), jax.ShapeDtypeStruct((4, FL, FL), F32), arr(FL, D), arr(D, D), arr(D, D),
            arr(D, FL), arr(D, FL), arr(8 * SH, FL), arr(D, FL),
            arr(8, PR, D), arr(8, PR, D), arr(8, PR, D),
            arr(4, QR, D), arr(4, QR, D), arr(4, QR, D), arr(4, QR, D), arr(4, QR, D),
            arr(PR, D), arr(PR, D),
        ]
        out = pl.pallas_call(
            kernel,
            name="backward",
            out_shape=outs,
            in_specs=[any_] * 5,
            out_specs=[any_] * len(outs),
            scratch_shapes=[
                vmem(FL, D), vmem(D, FL), vmem(D, FL), vmem(4, FL, FL, dtype=F32), vmem(4 * QR, D),
                vmem(PR + SH, D, dtype=F32), vmem(4 * QR, FL), vmem(4 * QR, FL), vmem(QR, D), vmem(QR, D),
                vmem(2 * SH, FL), vmem(2 * SH, FL), vmem(2 * SH, FL),
                *gather_sems, *gather_sems, dma((8,)), dma((8,)), dma((2,)),
                dma((8,)), dma((8,)), dma((8,)), dma((4,)), dma((4,)), dma((4,)), dma((4,)), dma((4,)), dma((2,)), dma((7,)),
            ],
            compiler_params=pltpu.CompilerParams(collective_id=0, has_side_effects=True, vmem_limit_bytes=VMEM),
        )(x, dy, pre, w_in, w_down)
        dx, acc, down, _, full, _, dpre = out[:7]
        dw_in, dw_down, dx = finish(acc, full, dpre, down, dx)
        return dx, dw_in, dw_down

    rows = P(("dp", "tp"), None)
    cols = P("dp", "tp")
    return jax.shard_map(
        step, mesh=mesh,
        in_specs=(rows, rows, cols, P(None, "tp"), P("tp", None)),
        out_specs=(rows, cols, rows),
        check_vma=False,
    )
```

time: 1360 us -> 489 us (0.36)
  waiting for transfers between devices: 831 us -> 0 us
  Pallas kernels: 0 us -> 485 us
  matrix products: 344 us -> 0 us
  local copies, waits for them, and re-layouts: 85.8 us -> 1.58 us
  starting transfers between devices: 59.3 us -> 0 us
  loops' own time: 14.5 us -> 0 us
    dot_general x34 -> x0, waiting for transfers between devices: 660 us -> none  [by_group(): jnp.einsum('gta,gtb->gab', a, b, preferred_element_type=jnp.float32)]
    pallas_call x0 -> x2, Pallas kernels: none -> 485 us  [the longest x1 463 us: step(): pl.pallas_call(kernel, name='backward', out_shape=outs, in_specs=[any_] *...]
    dot_general x18 -> x0, matrix products: 344 us -> none  [the longest x16 248 us: by_group(): jnp.einsum('gta,gtb->gab', a, b, preferred_element_type=jnp.float32)]
    unnamed x4 -> x0, waiting for transfers between devices: 171 us -> none
    dot_general x34 -> x0, starting transfers between devices: 59.2 us -> none  [by_group(): jnp.einsum('gta,gtb->gab', a, b, preferred_element_type=jnp.float32)]
    dot_general x25 -> x0, local copies, waits for them, and re-layouts: 56.5 us -> none
    unnamed x6 -> x2, local copies, waits for them, and re-layouts: 29.3 us -> 1.58 us
    another operation x2 -> x0, loops' own time: 14.5 us -> none  [by_group(): jnp.einsum('gta,gtb->gab', a, b, preferred_element_type=jnp.float32)]
  transfers between devices with their start and end apart: 36 -> 0, of which waited for: 27 -> 0; matrix products, arithmetic and copies ran while one was open for 25% -> 0% of each run, Pallas kernels for 0% -> 0%
where the time goes in v2:
time: 489 us; the launch traced here: 488 us
  Pallas kernels  485 us (99%)
    pallas_call x1, Pallas kernels, step(): pl.pallas_call(kernel, name='backward', out_shape=outs, in_specs=[any_] *...  463 us
    pallas_call x1, Pallas kernels, finish(): pl.pallas_call(place, name='finish', grid=(steps,), in_specs=[part, pl.Bl...  22.4 us

profile of v2, /device:TPU:0, one launch (start us, length us, event | category | flops | bytes accessed | tf_op | source)
XLA Modules:
  0.0 487.6 jit_solution(5597916907653062550)
XLA Ops:
  0.6 463.0 %backward.1 = (bf16[256,4096]{1,0:T(8,128)(2,1)}, f32[4,1024,1024]{2,1,0:T(8,128)}, bf16[1024,4096]{1,0:T(8,128)(2,1)}, bf16[4096,4096]{1,0:T(8,128)(2,1)}, bf16...) custom-call(bf16[256,4096]{1,0:T(8,128)(2,1)} %x.1, ...), custom_call_target="tpu_custom_call" | custom-call | tf_op jit(solution)/shard_map/backward/pallas_call | solution.py:594
  463.6 0.0 copy-start
  463.6 1.6 copy-done
  465.2 22.4 %finish.1 = (bf16[4096,1024]{1,0:T(8,128)(2,1)}, bf16[1024,4096]{1,0:T(8,128)(2,1)}, bf16[256,4096]{1,0:T(8,128)(2,1)}) custom-call(f32[4096,1024]{1,0:T(8,128)} %bitcast.1, bf16[4096,4096]{1,0:T(8,128)(2,1)} %get-tuple-element.12.x0.x1, bf16[4096,4096]{1,0:T(8,128)(2,1)} %get-tuple-element.12.x0.x1, bf16[4096,1024]{1,0:T(8,128)(2,1)} %get-tuple-element.13.dp0.dp1, ...), custom_call_target="tpu_custom_call" | custom-call | tf_op jit(solution)/shard_map/finish/pallas_call | solution.py:556
Async XLA Ops:
  463.6 1.6 copy-start

commit v3 on v2

--- a/solution.py
+++ b/solution.py
@@ -13,8 +13,8 @@
 D = 4096
 FL = 1024
 SH = 256
-CHUNKS_A = ((0, 128, "q"), (128, 128, "q"))
-CHUNKS_B = ((0, 112, "p"), (112, 80, "q"), (192, 64, "q"))
+CHUNKS_A = ((0, 16, "p"), (16, 80, "q"), (96, 80, "q"), (176, 80, "q"))
+CHUNKS_B = ((0, 128, "p"), (128, 64, "q"), (192, 64, "q"))
 PR = 80
 QR = 176
 VMEM = 66_000_000
@@ -299,6 +299,7 @@
     pairs(pair, 1, False)
     gy.step(1)
     gx.begin_z()
+    place_own(x, gx)
     gy.across(1)
     pairs(early, 1, True)
     gy.step(2)
@@ -467,14 +468,14 @@
         cp = rdma(dpre.at[pl.ds(0, SH)], dps.at[pl.ds(d * SH, SH)], dps_s.at[d], dps_r.at[d], other)
         cp.wait_recv()
         cp.wait_send()
+    gx.turn()
     load_wo.wait()
     load_ws.wait()
     q_terms()
     qy_copy(target(0)).start()
     qy_copy(target(1)).start()
-    gx.turn()
-    place_own(x, gx)
     towards(0, outer)
+    gx.step(0)
 
     def late_first(k, _):
         late(jnp.where(inner, 1 - y, jnp.where(k == 0, 1 - y, y)), z + inward * jnp.where(inner, 1 - 2 * k, 1 + k))
@@ -485,7 +486,6 @@
         return 0
 
     lax.fori_loop(0, 2, late_first, 0)
-    gx.step(0)
     gx.across(0)
     qy_copy(target(2)).start()
     towards(0, inner, (lambda: late(y, z + 2 * inward), lambda: late(1 - y, z + 2 * inward)))
@@ -502,17 +502,23 @@
     gx.across(1)
     gx.step(2)
     towards(2, inner)
+
+    def pass_over():
+        terms(z)
+        arrived(1 - y, 0)
+        store(pys_b, 0, PR)
+        py_copy().start()
+
     in_step(y, jnp.where(inner, z + 1, z + inward))
+    pl.when(inner)(pass_over)
     pairs(in_step, 1, True)
+    pl.when(outer)(pass_over)
     gx.across(2)
     in_step(y, z + 2 * inward, outer)
     in_step(1 - y, z + 2 * inward, outer)
     save = local(acc, acc_o, lsem.at[4])
     save.start()
     terms(z)
-    arrived(1 - y, 0)
-    store(pys_b, 0, PR)
-    py_copy().start()
     add(qy_b.at[z], qy_copy(z), 2 * PR, QR)
     arrived(None, 2 * PR)
     store(dx.at[pl.ds(PR, QR)], 2 * PR, QR)
@@ -567,7 +573,7 @@
         ],
         out_specs=[part, tall, flat],
         out_shape=[jax.ShapeDtypeStruct(s, BF16) for s in ((D, FL), (FL, D), (SH, D))],
-        compiler_params=pltpu.CompilerParams(vmem_limit_bytes=48_000_000),
+        compiler_params=pltpu.CompilerParams(vmem_limit_bytes=VMEM),
     )(acc.reshape(D, FL), full, full, dpre, dpre, down, dx)
 
 
@@ -581,7 +587,7 @@
     def vmem(*shape, dtype=BF16):
         return pltpu.VMEM(shape, dtype)
 
-    gather_sems = [dma((8, 3)), dma((2, 8, 3)), dma((8, 3)), dma((8,)), dma((8,))]
+    gather_sems = [dma((8, 4)), dma((2, 8, 4)), dma((8, 4)), dma((8,)), dma((8,))]
 
     def step(x, dy, pre, w_in, w_down):
         outs = [

time: 489 us -> 478 us (0.978)
  Pallas kernels: 485 us -> 476 us
    pallas_call x1, Pallas kernels: 463 us -> 453 us  [step(): pl.pallas_call(kernel, name='backward', out_shape=outs, in_specs=[any_] *...]
where the time goes in v3:
time: 478 us; the launch traced here: 477 us
  Pallas kernels  476 us (100%)
    pallas_call x1, Pallas kernels, step(): pl.pallas_call(kernel, name='backward', out_shape=outs, in_specs=[any_] *...  453 us
    pallas_call x1, Pallas kernels, finish(): pl.pallas_call(place, name='finish', grid=(steps,), in_specs=[part, pl.Bl...  22.8 us

profile of v3, /device:TPU:0, one launch (start us, length us, event | category | flops | bytes accessed | tf_op | source)
XLA Modules:
  0.0 476.9 jit_solution(4123254066989468489)
XLA Ops:
  0.6 453.4 %backward.1 = (bf16[256,4096]{1,0:T(8,128)(2,1)}, f32[4,1024,1024]{2,1,0:T(8,128)}, bf16[1024,4096]{1,0:T(8,128)(2,1)}, bf16[4096,4096]{1,0:T(8,128)(2,1)}, bf16...) custom-call(bf16[256,4096]{1,0:T(8,128)(2,1)} %x.1, ...), custom_call_target="tpu_custom_call" | custom-call | tf_op jit(solution)/shard_map/backward/pallas_call | solution.py:600
  454.1 22.8 %finish.1 = (bf16[4096,1024]{1,0:T(8,128)(2,1)}, bf16[1024,4096]{1,0:T(8,128)(2,1)}, bf16[256,4096]{1,0:T(8,128)(2,1)}) custom-call(f32[4096,1024]{1,0:T(8,128)} %bitcast.1, bf16[4096,4096]{1,0:T(8,128)(2,1)} %get-tuple-element.12.x0.x1, bf16[4096,4096]{1,0:T(8,128)(2,1)} %get-tuple-element.12.x0.x1, bf16[4096,1024]{1,0:T(8,128)(2,1)} %get-tuple-element.13.dp0.dp1, ...), custom_call_target="tpu_custom_call" | custom-call | tf_op jit(solution)/shard_map/finish/pallas_call | solution.py:562

commit v4 on v3

--- a/solution.py
+++ b/solution.py
@@ -324,11 +324,11 @@
         o = (0, 1, 5 - far, far)[i]
         return high * o + (1 - high) * (3 - o)
 
-    def fetch(ys, zs, r0, n, at):
+    def fetch(ys, zs, r0, n, at, sem=0):
         o = pl.multiple_of(tp_of(ys, zs, c) * SH + r0, 16)
         s = pl.multiple_of((ys * 4 + zs) * SH + r0, 16)
-        return (local(dpre.at[pl.ds(o, n)], a1.at[pl.ds(at, n)], lsem.at[0]),
-                local(dps.at[pl.ds(s, n)], a2.at[pl.ds(at, n)], lsem.at[1]))
+        return (local(dpre.at[pl.ds(o, n)], a1.at[pl.ds(at, n)], lsem.at[sem]),
+                local(dps.at[pl.ds(s, n)], a2.at[pl.ds(at, n)], lsem.at[sem + 1]))
 
     def fetch_all(parts):
         for part in parts:
@@ -349,7 +349,7 @@
         both(*(local(big.at[pl.ds(i * QR, QR)], qys_b.at[target(i)], lsem.at[i]) for i in range(4)))
 
     def terms(v):
-        fetch_all([fetch(1 - y, v, 0, PR, 0), fetch(y, v, 0, SH, PR)])
+        both(*fetch(1 - y, v, 0, PR, 0), *fetch(y, v, 0, SH, PR, 2))
         n = PR + SH
 
         def tile(j, _):

time: 478 us -> 476 us (level)
  no operation moved by 1% of the time
where the time goes in v4:
time: 476 us; the launch traced here: 474 us
  Pallas kernels  474 us (100%)
    pallas_call x1, Pallas kernels, step(): pl.pallas_call(kernel, name='backward', out_shape=outs, in_specs=[any_] *...  451 us
    pallas_call x1, Pallas kernels, finish(): pl.pallas_call(place, name='finish', grid=(steps,), in_specs=[part, pl.Bl...  22.8 us

profile of v4, /device:TPU:0, one launch (start us, length us, event | category | flops | bytes accessed | tf_op | source)
XLA Modules:
  0.0 474.4 jit_solution(13483127710501286257)
XLA Ops:
  0.6 450.9 %backward.1 = (bf16[256,4096]{1,0:T(8,128)(2,1)}, f32[4,1024,1024]{2,1,0:T(8,128)}, bf16[1024,4096]{1,0:T(8,128)(2,1)}, bf16[4096,4096]{1,0:T(8,128)(2,1)}, bf16...) custom-call(bf16[256,4096]{1,0:T(8,128)(2,1)} %x.1, ...), custom_call_target="tpu_custom_call" | custom-call | tf_op jit(solution)/shard_map/backward/pallas_call | solution.py:600
  451.6 22.8 %finish.1 = (bf16[4096,1024]{1,0:T(8,128)(2,1)}, bf16[1024,4096]{1,0:T(8,128)(2,1)}, bf16[256,4096]{1,0:T(8,128)(2,1)}) custom-call(f32[4096,1024]{1,0:T(8,128)} %bitcast.1, bf16[4096,4096]{1,0:T(8,128)(2,1)} %get-tuple-element.12.x0.x1, bf16[4096,4096]{1,0:T(8,128)(2,1)} %get-tuple-element.12.x0.x1, bf16[4096,1024]{1,0:T(8,128)(2,1)} %get-tuple-element.13.dp0.dp1, ...), custom_call_target="tpu_custom_call" | custom-call | tf_op jit(solution)/shard_map/finish/pallas_call | solution.py:562
